TPU v7x, 16 devices: a whole 2x2x2 slice. The times are simulated.
16 devices in a mesh: rep: 1, dp: 16 (over x, y, z, core).
Axes of the slice: x: 2, y: 2, z: 2, core: 2. Of those that a mesh axis runs over, the one named last changes fastest.
Arguments:
- x: bfloat16 [16, 2048, 1024], P(('rep', 'dp'))
- dy: bfloat16 [16, 2048, 1024], P(('rep', 'dp'))
- w_gate: bfloat16 [2, 1024, 2816], P(None, 'dp')
- w_up: bfloat16 [2, 1024, 2816], P(None, 'dp')
- w_down: bfloat16 [2, 2816, 1024], P(None, 'dp')
Outputs:
- output 1: bfloat16 [16, 2048, 1024], P(('rep', 'dp'))
- output 2: bfloat16 [2, 1024, 2816], P('rep', 'dp')
- output 3: bfloat16 [2, 1024, 2816], P('rep', 'dp')
- output 4: bfloat16 [2, 2816, 1024], P('rep', 'dp')
All inputs are finite; a program needn't handle non-finite values.
Results may differ from a plain program's by a relative error of at most 0.018.
Values are sent between devices in bfloat16 or wider.
A program may use at most 2 GiB of HBM per device.

v0:
```python
import jax
import jax.numpy as jnp
from jax import lax

NAMES = ("w_gate", "w_up", "w_down")


def matmul(a, w):
    return jnp.dot(a, w, preferred_element_type=jnp.float32).astype(jnp.bfloat16)


def normed(h):
    wide = h.astype(jnp.float32)
    scale = lax.rsqrt(jnp.mean(wide**2, -1, keepdims=True) + 1e-6)
    return (wide * scale).astype(jnp.bfloat16)


def layer(h, w):
    a = normed(h)
    gate = jnp.dot(a, w["w_gate"], preferred_element_type=jnp.float32)
    up = jnp.dot(a, w["w_up"], preferred_element_type=jnp.float32)
    return h + matmul((jax.nn.silu(gate) * up).astype(jnp.bfloat16), w["w_down"])


def stack(weights, h):
    for number in range(weights["w_gate"].shape[0]):
        h = layer(h, {name: w[number] for name, w in weights.items()})
    return h


def solution(mesh):
    groups = mesh.shape["rep"]

    def step(x, dy, *weights):
        shape = x.shape
        x, dy = (t.reshape(groups, -1, *t.shape[1:]) for t in (x, dy))

        def of_a_group(x, dy):
            _, back = jax.vjp(stack, dict(zip(NAMES, weights, strict=True)), x)
            by_weights, by_x = back(dy)
            return (by_x, *(by_weights[name] for name in NAMES))

        by_x, *by_weights = jax.vmap(of_a_group)(x, dy)
        return (by_x.reshape(shape), *(t.reshape(-1, *t.shape[2:]) for t in by_weights))

    return step
```

profile of v0, /device:TPU:0, one launch (start us, length us, event | category | flops | bytes accessed | tf_op | source)
XLA Modules:
  0.0 1501.4 jit_solution(9509849443852428824)
XLA Ops:
  42.2 133.9 %while.13 = (bf16[1,2048,1024]{2,1,0:T(8,128)(2,1)}, bf16[1,176,1024]{2,1,0:T(8,128)(2,1)S(1)}, bf16[1,2048,2816]{1,2,0:T(8,128)(2,1)}, bf16[1,176,1024]{2,1,0:T...) while((bf16[1,2048,1024]{2,1,0:T(8,128)(2,1)}, ...), condition=%wide.windowed_dot_general_cond_ag, body=%wide.windowed_dot_general_body_ag.sunk | while | flops 2953510912 | bytes 24248860 | solution.py:9
  102.1 12.5 collective-permute-done.3
  162.7 9.5 collective-permute-done.1
  176.1 15.2 %copy.2 = bf16[1,2048,2816]{2,1,0:T(8,128)(2,1)} copy(bf16[1,2048,2816]{1,2,0:T(8,128)(2,1)} %get-tuple-element.42) | data formatting | bytes 23068672 | tf_op jit(solution)/vmap(transpose(jvp()))/dot_general | solution.py:9
  191.3 20.1 %fusion.204 = f32[2048,2816]{1,0:T(8,128)} fusion(bf16[1,1024,2816]{2,1,0:T(8,128)(2,1)} %all-gather.27.cloned.1.call-done, bf16[1,2048,1024]{1,2,0:T(8,128)(2,1)} %fusion.187), kind=kOutput, calls=%fused_computation.257 | convolution fusion | flops 11811160064 | bytes 33030144 | tf_op jit(solution)/vmap(jvp())/dot_general | solution.py:20
  211.3 27.7 %fusion.176 = (bf16[1,2048,2816]{2,1,0:T(8,128)(2,1)}, f32[2048,2816]{1,0:T(8,128)}) fusion(f32[2048,2816]{1,0:T(8,128)} %fusion.204, bf16[1,1024,2816]{2,1,0:T(8,128)(2,1)} %all-gather.29.cloned.1.call-done, bf16[1,2048,1024]{1,2,0:T(8,128)(2,1)} %fusion.187), kind=kOutput, calls=%fused_computation.215 | convolution fusion | flops 11845763072 | bytes 67633152 | tf_op jit(solution)/vmap(jvp())/dot_general | solution.py:21
  239.0 15.1 %copy.6 = bf16[1,2048,2816]{1,2,0:T(8,128)(2,1)} copy(bf16[1,2048,2816]{2,1,0:T(8,128)(2,1)} %get-tuple-element.281) | data formatting | bytes 23068672
  254.1 19.6 %fusion.189 = (f32[2048]{0:T(1024)S(1)}, bf16[1,2048,1024]{1,2,0:T(8,128)(2,1)}) fusion(bf16[1,2048,1024]{1,2,0:T(8,128)(2,1)} %copy.1, bf16[1,2816,1024]{2,1,0:T(8,128)(2,1)} %all-gather.31.cloned.1.call-done, bf16[1,2048,2816]{2,1,0:T(8,128)(2,1)} %get-tuple-element.281), kind=kOutput, calls=%fused_computation.242 | convolution fusion | flops 11821643776 | bytes 25698304 | tf_op jit(solution)/vmap(jvp())/dot_general | solution.py:9
  280.5 20.3 %fusion.196 = f32[2048,2816]{1,0:T(8,128)} fusion(bf16[1,1024,2816]{2,1,0:T(8,128)(2,1)} %all-gather.33.cloned.1.call-done, bf16[1,2048,1024]{1,2,0:T(8,128)(2,1)} %fusion.190), kind=kOutput, calls=%fused_computation.249 | convolution fusion | flops 11811160064 | bytes 33030144 | tf_op jit(solution)/vmap(jvp())/dot_general | solution.py:20
  300.8 27.7 %fusion.170 = (bf16[1,2048,2816]{2,1,0:T(8,128)(2,1)}, f32[2048,2816]{1,0:T(8,128)}) fusion(f32[2048,2816]{1,0:T(8,128)} %fusion.196, bf16[1,1024,2816]{2,1,0:T(8,128)(2,1)} %all-gather.35.cloned.1.call-done, bf16[1,2048,1024]{1,2,0:T(8,128)(2,1)} %fusion.190), kind=kOutput, calls=%fused_computation.205 | convolution fusion | flops 11845763072 | bytes 67633152 | tf_op jit(solution)/vmap(jvp())/dot_general | solution.py:21
  328.5 15.3 %copy.4 = bf16[1,2048,2816]{1,2,0:T(8,128)(2,1)} copy(bf16[1,2048,2816]{2,1,0:T(8,128)(2,1)} %get-tuple-element.289) | data formatting | bytes 23068672
  343.8 149.1 %while.18 = (bf16[1,2048,2816]{1,2,0:T(8,128)(2,1)}, bf16[1,2048,1024]{2,1,0:T(8,128)(2,1)}, f32[176,1024]{1,0:T(8,128)S(1)}, f32[176,1024]{1,0:T(8,128)}, u32[]...) while((bf16[1,2048,2816]{1,2,0:T(8,128)(2,1)}, ...), condition=%wide.windowed_dot_general_cond_rs.4.clone, body=%wide.windowed_dot_general_body_rs.4.clone.sunk | while | flops 2959638528 | bytes 57410128 | solution.py:9
  357.6 14.5 collective-permute-start.22
  417.8 9.7 collective-permute-start.20
  437.4 7.8 collective-permute-start.22
  456.3 9.7 collective-permute-start.20
  492.9 9.6 collective-permute-start.33
  502.5 20.4 %convert_multiply_fusion.3 = (bf16[1,2048,2816]{2,1,0:T(8,128)(2,1)S(1)}, bf16[1,2048,2816]{2,1,0:T(8,128)(2,1)S(1)}) fusion(f32[2048,2816]{1,0:T(8,128)} %fusion.196, bf16[1,2048,2816]{2,1,0:T(8,128)(2,1)} %copy.2, f32[2048,2816]{1,0:T(8,128)} %get-tuple-element.290), kind=kLoop, calls=%fused_computation.193 | loop fusion | flops 86507520 | bytes 80740352 | tf_op jit(solution)/vmap(transpose(jvp()))/mul | solution.py:22
  522.9 16.8 %fusion.168 = bf16[2048,1024]{0,1:T(8,128)(2,1)} fusion(bf16[1,2048,2816]{2,1,0:T(8,128)(2,1)S(1)} %get-tuple-element.622, bf16[1,1024,2816]{2,1,0:T(8,128)(2,1)} %all-gather.33.cloned.1.call-done), kind=kOutput, calls=%fused_computation.202 | convolution fusion | flops 11811160064 | bytes 21495808 | tf_op jit(solution)/vmap(transpose(jvp()))/dot_general | solution.py:20
  539.7 17.3 %fusion.191 = (f32[2048]{0:T(1024)S(1)}, bf16[2048,1024]{0,1:T(8,128)(2,1)}) fusion(bf16[1,2048,1024]{1,2,0:T(8,128)(2,1)} %get-tuple-element.284, bf16[2048,1024]{0,1:T(8,128)(2,1)} %fusion.168, bf16[1,1024,2816]{2,1,0:T(8,128)(2,1)} %all-gather.35.cloned.1.call-done, bf16[1,2048,2816]{2,1,0:T(8,128)(2,1)S(1)} %get-tuple-element.694), kind=kOutput, calls=%fused_computation.244 | convolution fusion | flops 11821643776 | bytes 29892608 | tf_op jit(solution)/vmap(transpose(jvp()))/dot_general | solution.py:21
  571.1 149.5 %while.19 = (bf16[1,2048,1024]{2,1,0:T(8,128)(2,1)}, bf16[1,2048,2816]{1,2,0:T(8,128)(2,1)}, f32[1024,176]{0,1:T(8,128)S(1)}, f32[1024,176]{0,1:T(8,128)}, u32[]...) while((bf16[1,2048,1024]{2,1,0:T(8,128)(2,1)}, ...), condition=%wide.windowed_dot_general_cond_rs.5.clone, body=%wide.windowed_dot_general_body_rs.5.clone.sunk | while | flops 2959638528 | bytes 57410128 | solution.py:9
  584.7 14.5 collective-permute-start.26
  645.5 9.7 collective-permute-start.24
  683.1 9.7 collective-permute-start.24
  702.8 7.9 collective-permute-start.26
  720.5 9.6 collective-permute-start.34
  730.2 161.1 %while.16 = (bf16[1,2048,2816]{2,1,0:T(8,128)(2,1)}, bf16[1,2048,1024]{1,2,0:T(8,128)(2,1)}, f32[2816,64]{0,1:T(8,128)}, f32[2816,64]{0,1:T(8,128)}, u32[]{:T(12...) while((bf16[1,2048,2816]{2,1,0:T(8,128)(2,1)}, ...), condition=%wide.windowed_dot_general_cond_rs.2.clone, body=%wide.windowed_dot_general_body_rs.2.clone.sunk | while | flops 2955968512 | bytes 108790456 | solution.py:21
  746.2 14.5 collective-permute-start.14
  812.4 8.9 collective-permute-start.12
  891.3 9.1 collective-permute-start.31
  900.4 33.9 %convert_multiply_fusion.1 = (bf16[1,2048,2816]{2,1,0:T(8,128)(2,1)}, bf16[1,2048,2816]{2,1,0:T(8,128)(2,1)}) fusion(f32[2048,2816]{1,0:T(8,128)} %fusion.204, f32[2048,2816]{1,0:T(8,128)} %get-tuple-element.282, bf16[1,2816,1024]{2,1,0:T(8,128)(2,1)} %all-gather.31.cloned.1.call-done, bf16[1,2048,1024]{1,2,0:T(8,128)(2,1)} %fusion.207), kind=kOutput, calls=%fused_computation.191 | convolution fusion | flops 11903434752 | bytes 79167488 | tf_op jit(solution)/vmap(transpose(jvp()))/dot_general | solution.py:9
  934.2 160.5 %while.17 = (bf16[1,2048,2816]{2,1,0:T(8,128)(2,1)}, bf16[1,2048,1024]{1,2,0:T(8,128)(2,1)}, f32[2816,64]{0,1:T(8,128)}, f32[2816,64]{0,1:T(8,128)}, u32[]{:T(12...) while((bf16[1,2048,2816]{2,1,0:T(8,128)(2,1)}, ...), condition=%wide.windowed_dot_general_cond_rs.3.clone, body=%wide.windowed_dot_general_body_rs.3.clone.sunk | while | flops 2955968512 | bytes 108790456 | solution.py:21
  950.1 14.6 collective-permute-start.18
  1055.8 8.9 collective-permute-start.16
  1094.8 160.3 %while.14 = (bf16[1,2048,2816]{2,1,0:T(8,128)(2,1)}, bf16[1,2048,1024]{1,2,0:T(8,128)(2,1)}, f32[2816,64]{0,1:T(8,128)}, f32[2816,64]{0,1:T(8,128)}, u32[]{:T(12...) while((bf16[1,2048,2816]{2,1,0:T(8,128)(2,1)}, ...), condition=%wide.windowed_dot_general_cond_rs.clone, body=%wide.windowed_dot_general_body_rs.clone.sunk | while | flops 2955968512 | bytes 108790456 | solution.py:20
  1114.5 8.8 collective-permute-start.6
  1135.4 8.7 collective-permute-start.4
  1176.4 8.7 collective-permute-start.4
  1217.3 7.8 collective-permute-start.4
  1255.1 161.4 %while.15 = (bf16[1,2048,2816]{2,1,0:T(8,128)(2,1)}, bf16[1,2048,1024]{1,2,0:T(8,128)(2,1)}, f32[2816,64]{0,1:T(8,128)}, f32[2816,64]{0,1:T(8,128)}, u32[]{:T(12...) while((bf16[1,2048,2816]{2,1,0:T(8,128)(2,1)}, ...), condition=%wide.windowed_dot_general_cond_rs.1.clone, body=%wide.windowed_dot_general_body_rs.1.clone.sunk | while | flops 2955968512 | bytes 108790456 | solution.py:20
  1256.0 8.7 collective-permute-start.8
  1275.9 8.8 collective-permute-start.10
  1296.9 8.7 collective-permute-start.8
  1337.8 7.8 collective-permute-start.8
  1377.7 8.7 collective-permute-start.8
  1416.5 8.8 collective-permute-start.32
  1425.2 18.3 %fusion.164 = bf16[2048,1024]{0,1:T(8,128)(2,1)} fusion(bf16[1,2048,2816]{2,1,0:T(8,128)(2,1)} %get-tuple-element.810, bf16[1,1024,2816]{2,1,0:T(8,128)(2,1)} %all-gather.27.cloned.1.call-done), kind=kOutput, calls=%fused_computation.198 | convolution fusion | flops 11811160064 | bytes 21495808 | tf_op jit(solution)/vmap(transpose(jvp()))/dot_general | solution.py:20
  1443.6 16.4 %fusion.188 = (f32[2048]{0:T(1024)S(1)}, bf16[2048,1024]{0,1:T(8,128)(2,1)}) fusion(bf16[1,2048,1024]{1,2,0:T(8,128)(2,1)S(1)} %copy-done.6, bf16[2048,1024]{0,1:T(8,128)(2,1)} %fusion.164, bf16[1,1024,2816]{2,1,0:T(8,128)(2,1)} %all-gather.29.cloned.1.call-done, bf16[1,2048,2816]{2,1,0:T(8,128)(2,1)S(1)} %bitcast.592), kind=kOutput, calls=%fused_computation.241 | convolution fusion | flops 11821643776 | bytes 29892608 | tf_op jit(solution)/vmap(transpose(jvp()))/dot_general | solution.py:21
  (627 shorter events, 934.6 us)
Async XLA Ops:
  7.2 184.1 %all-gather.27.cloned.1.call-start = ((), (), s32[]{:S(2)}) async-start(), calls=%async_computation | async-start | bytes 6127616 | tf_op jit(solution)/vmap(jvp())/squeeze | solution.py:27
  9.2 202.1 %all-gather.29.cloned.1.call-start = ((), (), s32[]{:S(2)}) async-start(), calls=%async_computation.1 | async-start | bytes 6127616 | tf_op jit(solution)/vmap(jvp())/squeeze | solution.py:27
  11.3 242.8 %all-gather.31.cloned.1.call-start = ((), (), s32[]{:S(2)}) async-start(), calls=%async_computation.2 | async-start | bytes 6127616 | tf_op jit(solution)/vmap(jvp())/squeeze | solution.py:27
  13.3 267.2 %all-gather.33.cloned.1.call-start = ((), (), s32[]{:S(2)}) async-start(), calls=%async_computation.3 | async-start | bytes 6127616 | tf_op jit(solution)/vmap(jvp())/squeeze | solution.py:27
  13.9 287.0 %all-gather.35.cloned.1.call-start = ((), (), s32[]{:S(2)}) async-start(), calls=%async_computation.4 | async-start | bytes 6127616 | tf_op jit(solution)/vmap(jvp())/squeeze | solution.py:27
  13.9 22.5 %collective-permute-start.28 = (bf16[1,176,1024]{2,1,0:T(8,128)(2,1)S(1)}, bf16[1,176,1024]{2,1,0:T(8,128)(2,1)S(1)}, u32[]{:S(2)}, u32[]{:S(2)}) collective-permute-start(bf16[1,176,1024]{2,1,0:T(8,128)(2,1)S(1)} %get-tuple-element.557), channel_id=6, source_target_pairs={{0,1},{1,2},{2,3},{3,4},{4,5},{5,6},{6,7},{7,8},{8,9},{9,10},{10,1... | collective-permute-start | bytes 1081352 | tf_op jit(solution)/vmap(transpose(jvp()))/dot_general | solution.py:9
  73.5 14.8 collective-permute-start.2
  93.7 21.0 %collective-permute-start.3 = (bf16[1,176,1024]{2,1,0:T(8,128)(2,1)S(1)}, bf16[1,176,1024]{2,1,0:T(8,128)(2,1)S(1)}, u32[]{:S(2)}, u32[]{:S(2)}) collective-permute-start(bf16[1,176,1024]{2,1,0:T(8,128)(2,1)S(1)} %collective-permute-done.2), channel_id=10, source_target_pairs={{0,1},{1,2},{2,3},{3,4},{4,5},{5,6},{6,7},{7,8},{8,9},{9,10},{10,1... | collective-permute-start | bytes 1081352 | tf_op jit(solution)/vmap(transpose(jvp()))/dot_general | solution.py:9
  139.3 15.4 %collective-permute-start.2 = (bf16[1,176,1024]{2,1,0:T(8,128)(2,1)S(1)}, bf16[1,176,1024]{2,1,0:T(8,128)(2,1)S(1)}, u32[]{:S(2)}, u32[]{:S(2)}) collective-permute-start(bf16[1,176,1024]{2,1,0:T(8,128)(2,1)S(1)} %get-tuple-element.569), channel_id=8, source_target_pairs={{0,1},{1,2},{2,3},{3,4},{4,5},{5,6},{6,7},{7,8},{8,9},{9,10},{10,1... | collective-permute-start | bytes 1081352 | tf_op jit(solution)/vmap(transpose(jvp()))/dot_general | solution.py:9
  159.6 16.5 %collective-permute-start.3 = (bf16[1,176,1024]{2,1,0:T(8,128)(2,1)S(1)}, bf16[1,176,1024]{2,1,0:T(8,128)(2,1)S(1)}, u32[]{:S(2)}, u32[]{:S(2)}) collective-permute-start(bf16[1,176,1024]{2,1,0:T(8,128)(2,1)S(1)} %collective-permute-done.2), channel_id=10, source_target_pairs={{0,1},{1,2},{2,3},{3,4},{4,5},{5,6},{6,7},{7,8},{8,9},{9,10},{10,1... | collective-permute-start | bytes 1081352 | tf_op jit(solution)/vmap(transpose(jvp()))/dot_general | solution.py:9
  357.6 18.8 %collective-permute-start.22 = (f32[176,1024]{1,0:T(8,128)S(1)}, f32[176,1024]{1,0:T(8,128)S(1)}, u32[]{:S(2)}, u32[]{:S(2)}) collective-permute-start(f32[176,1024]{1,0:T(8,128)S(1)} %get-tuple-element.543), channel_id=45, source_target_pairs={{0,1},{1,2},{2,3},{3,4},{4,5},{5,6},{6,7},{7,8},{8,9},{9,10},{10,1... | collective-permute-start | bytes 2162696 | tf_op jit(solution)/vmap(transpose(jvp()))/dot_general | solution.py:9
  383.2 12.7 collective-permute-start.20
  399.5 12.7 collective-permute-start.22
  417.8 14.9 collective-permute-start.20
  437.4 12.7 collective-permute-start.22
  456.3 14.9 collective-permute-start.20
  476.0 12.7 collective-permute-start.22
  492.9 983.8 %collective-permute-start.33 = (f32[176,1024]{1,0:T(8,128)}, f32[176,1024]{1,0:T(8,128)}, u32[]{:S(2)}, u32[]{:S(2)}) collective-permute-start(f32[176,1024]{1,0:T(8,128)} %get-tuple-element.52), channel_id=46, source_target_pairs={{0,1},{1,2},{2,3},{3,4},{4,5},{5,6},{6,7},{7,8},{8,9},{9,10},{10,1... | collective-permute-start | bytes 2162696 | tf_op jit(solution)/vmap(transpose(jvp()))/dot_general | solution.py:9
  584.7 18.8 %collective-permute-start.26 = (f32[1024,176]{0,1:T(8,128)S(1)}, f32[1024,176]{0,1:T(8,128)S(1)}, u32[]{:S(2)}, u32[]{:S(2)}) collective-permute-start(f32[1024,176]{0,1:T(8,128)S(1)} %get-tuple-element.552), channel_id=51, source_target_pairs={{0,1},{1,2},{2,3},{3,4},{4,5},{5,6},{6,7},{7,8},{8,9},{9,10},{10,1... | collective-permute-start | bytes 2162696 | tf_op jit(solution)/vmap(transpose(jvp()))/dot_general | solution.py:9
  610.3 12.7 collective-permute-start.24
  645.5 14.9 collective-permute-start.24
  665.1 12.7 collective-permute-start.26
  683.1 14.9 collective-permute-start.24
  702.8 12.7 collective-permute-start.26
  720.5 759.8 %collective-permute-start.34 = (f32[1024,176]{0,1:T(8,128)}, f32[1024,176]{0,1:T(8,128)}, u32[]{:S(2)}, u32[]{:S(2)}) collective-permute-start(f32[1024,176]{0,1:T(8,128)} %get-tuple-element.54), channel_id=52, source_target_pairs={{0,1},{1,2},{2,3},{3,4},{4,5},{5,6},{6,7},{7,8},{8,9},{9,10},{10,1... | collective-permute-start | bytes 2162696 | tf_op jit(solution)/vmap(transpose(jvp()))/dot_general | solution.py:9
  746.2 16.4 %collective-permute-start.14 = (f32[2816,64]{0,1:T(8,128)S(1)}, f32[2816,64]{0,1:T(8,128)S(1)}, u32[]{:S(2)}, u32[]{:S(2)}) collective-permute-start(f32[2816,64]{0,1:T(8,128)S(1)} %get-tuple-element.525), channel_id=33, source_target_pairs={{0,1},{1,2},{2,3},{3,4},{4,5},{5,6},{6,7},{7,8},{8,9},{9,10},{10,1... | collective-permute-start | bytes 2162696 | tf_op jit(solution)/vmap(transpose(jvp()))/dot_general | solution.py:21
  773.1 15.4 %collective-permute-start.12 = (f32[2816,64]{0,1:T(8,128)}, f32[2816,64]{0,1:T(8,128)}, u32[]{:S(2)}, u32[]{:S(2)}) collective-permute-start(f32[2816,64]{0,1:T(8,128)} %broadcast_select_fusion.28), channel_id=31, source_target_pairs={{0,1},{1,2},{2,3},{3,4},{4,5},{5,6},{6,7},{7,8},{8,9},{9,10},{10,1... | collective-permute-start | bytes 2162696 | tf_op jit(solution)/vmap(transpose(jvp()))/dot_general | solution.py:21
  792.5 12.7 collective-permute-start.14
  812.4 17.2 %collective-permute-start.12 = (f32[2816,64]{0,1:T(8,128)}, f32[2816,64]{0,1:T(8,128)}, u32[]{:S(2)}, u32[]{:S(2)}) collective-permute-start(f32[2816,64]{0,1:T(8,128)} %broadcast_select_fusion.28), channel_id=31, source_target_pairs={{0,1},{1,2},{2,3},{3,4},{4,5},{5,6},{6,7},{7,8},{8,9},{9,10},{10,1... | collective-permute-start | bytes 2162696 | tf_op jit(solution)/vmap(transpose(jvp()))/dot_general | solution.py:21
  853.6 15.9 %collective-permute-start.12 = (f32[2816,64]{0,1:T(8,128)}, f32[2816,64]{0,1:T(8,128)}, u32[]{:S(2)}, u32[]{:S(2)}) collective-permute-start(f32[2816,64]{0,1:T(8,128)} %broadcast_select_fusion.28), channel_id=31, source_target_pairs={{0,1},{1,2},{2,3},{3,4},{4,5},{5,6},{6,7},{7,8},{8,9},{9,10},{10,1... | collective-permute-start | bytes 2162696 | tf_op jit(solution)/vmap(transpose(jvp()))/dot_general | solution.py:21
  873.5 12.7 collective-permute-start.14
  891.3 586.7 %collective-permute-start.31 = (f32[2816,64]{0,1:T(8,128)}, f32[2816,64]{0,1:T(8,128)}, u32[]{:S(2)}, u32[]{:S(2)}) collective-permute-start(f32[2816,64]{0,1:T(8,128)} %get-tuple-element.48), channel_id=34, source_target_pairs={{0,1},{1,2},{2,3},{3,4},{4,5},{5,6},{6,7},{7,8},{8,9},{9,10},{10,1... | collective-permute-start | bytes 2162696 | tf_op jit(solution)/vmap(transpose(jvp()))/dot_general | solution.py:21
  950.1 16.4 %collective-permute-start.18 = (f32[2816,64]{0,1:T(8,128)S(1)}, f32[2816,64]{0,1:T(8,128)S(1)}, u32[]{:S(2)}, u32[]{:S(2)}) collective-permute-start(f32[2816,64]{0,1:T(8,128)S(1)} %get-tuple-element.534), channel_id=39, source_target_pairs={{0,1},{1,2},{2,3},{3,4},{4,5},{5,6},{6,7},{7,8},{8,9},{9,10},{10,1... | collective-permute-start | bytes 2162696 | tf_op jit(solution)/vmap(transpose(jvp()))/dot_general | solution.py:21
  976.9 15.4 %collective-permute-start.16 = (f32[2816,64]{0,1:T(8,128)}, f32[2816,64]{0,1:T(8,128)}, u32[]{:S(2)}, u32[]{:S(2)}) collective-permute-start(f32[2816,64]{0,1:T(8,128)} %broadcast_select_fusion.30), channel_id=37, source_target_pairs={{0,1},{1,2},{2,3},{3,4},{4,5},{5,6},{6,7},{7,8},{8,9},{9,10},{10,1... | collective-permute-start | bytes 2162696 | tf_op jit(solution)/vmap(transpose(jvp()))/dot_general | solution.py:21
  1016.0 15.9 %collective-permute-start.16 = (f32[2816,64]{0,1:T(8,128)}, f32[2816,64]{0,1:T(8,128)}, u32[]{:S(2)}, u32[]{:S(2)}) collective-permute-start(f32[2816,64]{0,1:T(8,128)} %broadcast_select_fusion.30), channel_id=37, source_target_pairs={{0,1},{1,2},{2,3},{3,4},{4,5},{5,6},{6,7},{7,8},{8,9},{9,10},{10,1... | collective-permute-start | bytes 2162696 | tf_op jit(solution)/vmap(transpose(jvp()))/dot_general | solution.py:21
  1036.0 12.7 collective-permute-start.18
  1055.8 17.2 %collective-permute-start.16 = (f32[2816,64]{0,1:T(8,128)}, f32[2816,64]{0,1:T(8,128)}, u32[]{:S(2)}, u32[]{:S(2)}) collective-permute-start(f32[2816,64]{0,1:T(8,128)} %broadcast_select_fusion.30), channel_id=37, source_target_pairs={{0,1},{1,2},{2,3},{3,4},{4,5},{5,6},{6,7},{7,8},{8,9},{9,10},{10,1... | collective-permute-start | bytes 2162696 | tf_op jit(solution)/vmap(transpose(jvp()))/dot_general | solution.py:21
  1077.0 12.7 collective-permute-start.18
  1095.6 14.8 collective-permute-start.4
  1135.4 17.1 %collective-permute-start.4 = (f32[2816,64]{0,1:T(8,128)}, f32[2816,64]{0,1:T(8,128)}, u32[]{:S(2)}, u32[]{:S(2)}) collective-permute-start(f32[2816,64]{0,1:T(8,128)} %broadcast_select_fusion.24), channel_id=19, source_target_pairs={{0,1},{1,2},{2,3},{3,4},{4,5},{5,6},{6,7},{7,8},{8,9},{9,10},{10,1... | collective-permute-start | bytes 2162696 | tf_op jit(solution)/vmap(transpose(jvp()))/dot_general | solution.py:20
  1176.4 17.0 %collective-permute-start.4 = (f32[2816,64]{0,1:T(8,128)}, f32[2816,64]{0,1:T(8,128)}, u32[]{:S(2)}, u32[]{:S(2)}) collective-permute-start(f32[2816,64]{0,1:T(8,128)} %broadcast_select_fusion.24), channel_id=19, source_target_pairs={{0,1},{1,2},{2,3},{3,4},{4,5},{5,6},{6,7},{7,8},{8,9},{9,10},{10,1... | collective-permute-start | bytes 2162696 | tf_op jit(solution)/vmap(transpose(jvp()))/dot_general | solution.py:20
  1217.3 16.1 %collective-permute-start.4 = (f32[2816,64]{0,1:T(8,128)}, f32[2816,64]{0,1:T(8,128)}, u32[]{:S(2)}, u32[]{:S(2)}) collective-permute-start(f32[2816,64]{0,1:T(8,128)} %broadcast_select_fusion.24), channel_id=19, source_target_pairs={{0,1},{1,2},{2,3},{3,4},{4,5},{5,6},{6,7},{7,8},{8,9},{9,10},{10,1... | collective-permute-start | bytes 2162696 | tf_op jit(solution)/vmap(transpose(jvp()))/dot_general | solution.py:20
  1256.0 15.9 %collective-permute-start.8 = (f32[2816,64]{0,1:T(8,128)}, f32[2816,64]{0,1:T(8,128)}, u32[]{:S(2)}, u32[]{:S(2)}) collective-permute-start(f32[2816,64]{0,1:T(8,128)} %broadcast_select_fusion.26), channel_id=25, source_target_pairs={{0,1},{1,2},{2,3},{3,4},{4,5},{5,6},{6,7},{7,8},{8,9},{9,10},{10,1... | collective-permute-start | bytes 2162696 | tf_op jit(solution)/vmap(transpose(jvp()))/dot_general | solution.py:20
  1296.9 17.0 %collective-permute-start.8 = (f32[2816,64]{0,1:T(8,128)}, f32[2816,64]{0,1:T(8,128)}, u32[]{:S(2)}, u32[]{:S(2)}) collective-permute-start(f32[2816,64]{0,1:T(8,128)} %broadcast_select_fusion.26), channel_id=25, source_target_pairs={{0,1},{1,2},{2,3},{3,4},{4,5},{5,6},{6,7},{7,8},{8,9},{9,10},{10,1... | collective-permute-start | bytes 2162696 | tf_op jit(solution)/vmap(transpose(jvp()))/dot_general | solution.py:20
  1337.8 16.1 %collective-permute-start.8 = (f32[2816,64]{0,1:T(8,128)}, f32[2816,64]{0,1:T(8,128)}, u32[]{:S(2)}, u32[]{:S(2)}) collective-permute-start(f32[2816,64]{0,1:T(8,128)} %broadcast_select_fusion.26), channel_id=25, source_target_pairs={{0,1},{1,2},{2,3},{3,4},{4,5},{5,6},{6,7},{7,8},{8,9},{9,10},{10,1... | collective-permute-start | bytes 2162696 | tf_op jit(solution)/vmap(transpose(jvp()))/dot_general | solution.py:20
  1377.7 17.0 %collective-permute-start.8 = (f32[2816,64]{0,1:T(8,128)}, f32[2816,64]{0,1:T(8,128)}, u32[]{:S(2)}, u32[]{:S(2)}) collective-permute-start(f32[2816,64]{0,1:T(8,128)} %broadcast_select_fusion.26), channel_id=25, source_target_pairs={{0,1},{1,2},{2,3},{3,4},{4,5},{5,6},{6,7},{7,8},{8,9},{9,10},{10,1... | collective-permute-start | bytes 2162696 | tf_op jit(solution)/vmap(transpose(jvp()))/dot_general | solution.py:20
  1416.5 62.7 %collective-permute-start.32 = (f32[2816,64]{0,1:T(8,128)}, f32[2816,64]{0,1:T(8,128)}, u32[]{:S(2)}, u32[]{:S(2)}) collective-permute-start(f32[2816,64]{0,1:T(8,128)} %get-tuple-element.50), channel_id=40, source_target_pairs={{0,1},{1,2},{2,3},{3,4},{4,5},{5,6},{6,7},{7,8},{8,9},{9,10},{10,1... | collective-permute-start | bytes 2162696 | tf_op jit(solution)/vmap(transpose(jvp()))/dot_general | solution.py:21
  1476.7 17.1 %collective-permute-start.30 = (f32[2816,64]{0,1:T(8,128)}, f32[2816,64]{0,1:T(8,128)S(1)}, u32[]{:S(2)}, u32[]{:S(2)}) collective-permute-start(f32[2816,64]{0,1:T(8,128)} %get-tuple-element.46), channel_id=28, source_target_pairs={{0,1},{1,2},{2,3},{3,4},{4,5},{5,6},{6,7},{7,8},{8,9},{9,10},{10,1... | collective-permute-start | bytes 2162696 | tf_op jit(solution)/vmap(transpose(jvp()))/dot_general | solution.py:20
  (164 other events, 2388.3 us)
Sparse Core Ops, SparseCore 0:
  10.2 51.4 all-gather.26
  63.9 56.4 all-gather.28
  122.6 58.5 all-gather.30
  183.3 40.2 all-gather.32
  225.6 40.1 all-gather.34
where the time goes:
time: 1510 us; the launch traced here: 1500 us
  starting transfers between devices  466 us (31%)
  matrix products  444 us (29%)
  waiting for transfers between devices  292 us (19%)
  other arithmetic  183 us (12%)
  local copies, waits for them, and re-layouts  99.6 us (7%)
    dot_general x51, starting transfers between devices, matmul(): jnp.dot(a, w, preferred_element_type=jnp.float32).astype(jnp.bfloat16)  185 us
    dot_general x26, matrix products, matmul(): jnp.dot(a, w, preferred_element_type=jnp.float32).astype(jnp.bfloat16)  153 us
    dot_general x20, matrix products, layer(): up = jnp.dot(a, w['w_up'], preferred_element_type=jnp.float32)  152 us
    dot_general x34, starting transfers between devices, layer(): up = jnp.dot(a, w['w_up'], preferred_element_type=jnp.float32)  147 us
    dot_general x20, matrix products, layer(): gate = jnp.dot(a, w['w_gate'], preferred_element_type=jnp.float32)  139 us
    dot_general x34, starting transfers between devices, layer(): gate = jnp.dot(a, w['w_gate'], preferred_element_type=jnp.float32)  134 us
    dot_general x51, waiting for transfers between devices, matmul(): jnp.dot(a, w, preferred_element_type=jnp.float32).astype(jnp.bfloat16)  127 us
    dot_general x34, waiting for transfers between devices, layer(): gate = jnp.dot(a, w['w_gate'], preferred_element_type=jnp.float32)  87.2 us
  transfers between devices with their start and end apart: 124, of which 91 were waited for; matrix products, arithmetic and copies ran while one was open for 45% of the time, Pallas kernels for 0%

commit v1 on v0

v1 whole, which is shorter than its diff:
```python
import jax
import jax.numpy as jnp
from jax import lax
from jax.sharding import PartitionSpec as P

F32, BF16 = jnp.float32, jnp.bfloat16
EPS = 1e-6


def dot(a, b, dims):
    return lax.dot_general(a, b, (dims, ((), ())), preferred_element_type=F32)


NN, NT, TN = ((1,), (0,)), ((1,), (1,)), ((0,), (0,))


def normed(h):
    wide = h.astype(F32)
    scale = lax.rsqrt(jnp.mean(wide**2, -1, keepdims=True) + EPS)
    return (wide * scale).astype(BF16)


def norm_back(h, da, dy):
    wide, d = h.astype(F32), da.astype(F32)
    scale = lax.rsqrt(jnp.mean(wide**2, -1, keepdims=True) + EPS)
    through = jnp.sum(d * wide, -1, keepdims=True)
    dh = d * scale - wide * (scale**3 * through / h.shape[-1])
    return dy + dh.astype(BF16)


def gated(gate, up):
    return (gate * jax.nn.sigmoid(gate) * up).astype(BF16)


def gated_back(gate, up, dhid):
    d, s = dhid.astype(F32), jax.nn.sigmoid(gate)
    dgate = d * up * (s * (1 + gate * (1 - s)))
    return dgate.astype(BF16), (d * gate * s).astype(BF16)


def gather(w):
    return lax.all_gather(w, "dp", axis=0, tiled=True)


def scatter(g):
    return lax.psum_scatter(g, "dp", scatter_dimension=0, tiled=True)


def device_step(x, dy, w_gate, w_up, w_down):
    x, dy = x[0], dy[0]
    wg0, wu0, wd0 = gather(w_gate[0]), gather(w_up[0]), gather(w_down[0])
    wd1, wg1, wu1 = gather(w_down[1]), gather(w_gate[1]), gather(w_up[1])

    a0 = normed(x)
    gate0, up0 = dot(a0, wg0, NN), dot(a0, wu0, NN)
    hid0 = gated(gate0, up0)
    h1 = x + dot(hid0, wd0, NN).astype(BF16)

    dhid1 = dot(dy, wd1, NT).astype(BF16)
    a1 = normed(h1)
    gate1, up1 = dot(a1, wg1, NN), dot(a1, wu1, NN)
    hid1 = gated(gate1, up1)
    dgate1, dup1 = gated_back(gate1, up1, dhid1)

    gd1 = scatter(dot(hid1, dy, TN).astype(BF16))
    gg1 = scatter(dot(a1, dgate1, TN).astype(BF16))
    gu1 = scatter(dot(a1, dup1, TN).astype(BF16))
    da1 = (dot(dgate1, wg1, NT) + dot(dup1, wu1, NT)).astype(BF16)
    dh1 = norm_back(h1, da1, dy)

    dhid0 = dot(dh1, wd0, NT).astype(BF16)
    dgate0, dup0 = gated_back(gate0, up0, dhid0)
    gd0 = scatter(dot(hid0, dh1, TN).astype(BF16))
    gg0 = scatter(dot(a0, dgate0, TN).astype(BF16))
    gu0 = scatter(dot(a0, dup0, TN).astype(BF16))
    da0 = (dot(dgate0, wg0, NT) + dot(dup0, wu0, NT)).astype(BF16)
    dx = norm_back(x, da0, dh1)
    return dx[None], jnp.stack([gg0, gg1]), jnp.stack([gu0, gu1]), jnp.stack([gd0, gd1])


def solution(mesh):
    tokens, rows = P(("rep", "dp"), None, None), P(None, "dp", None)
    return jax.shard_map(
        device_step,
        mesh=mesh,
        in_specs=(tokens, tokens, rows, rows, rows),
        out_specs=(tokens, P("rep", "dp", None), P("rep", "dp", None), P("rep", "dp", None)),
        check_vma=False,
    )
```

time: 1510 us -> 767 us (0.51)
  starting transfers between devices: 466 us -> 0.49 us
  other arithmetic: 183 us -> 17.1 us
  matrix products: 444 us -> 366 us
  local copies, waits for them, and re-layouts: 99.6 us -> 28 us
  waiting for transfers between devices: 292 us -> 331 us
    dot_general x119 -> x0, starting transfers between devices: 466 us -> none  [the longest x51 185 us: matmul(): jnp.dot(a, w, preferred_element_type=jnp.float32).astype(jnp.bfloat16)]
    dot_general x119 -> x0, waiting for transfers between devices: 291 us -> none  [the longest x51 127 us: matmul(): jnp.dot(a, w, preferred_element_type=jnp.float32).astype(jnp.bfloat16)]
    reduce_scatter x0 -> x6, waiting for transfers between devices: none -> 194 us  [scatter(): return lax.psum_scatter(g, 'dp', scatter_dimension=0, tiled=True)]
    all_gather x0 -> x6, waiting for transfers between devices: none -> 136 us  [gather(): return lax.all_gather(w, 'dp', axis=0, tiled=True)]
    dot_general x112 -> x0, other arithmetic: 126 us -> none
    dot_general x66 -> x17, matrix products: 444 us -> 366 us  [dot(): return lax.dot_general(a, b, (dims, ((), ())), preferred_element_type=F32)]
    dot_general x146 -> x0, local copies, waits for them, and re-layouts: 36.1 us -> none  [the longest x18 35.9 us: matmul(): jnp.dot(a, w, preferred_element_type=jnp.float32).astype(jnp.bfloat16)]
    unnamed x54 -> x27, local copies, waits for them, and re-layouts: 57.6 us -> 22 us
  transfers between devices with their start and end apart: 124 -> 12, of which waited for: 91 -> 9; matrix products, arithmetic and copies ran while one was open for 45% -> 45% of each run, Pallas kernels for 0% -> 0%
where the time goes in v1:
time: 767 us; the launch traced here: 757 us
  matrix products  366 us (48%)
  waiting for transfers between devices  331 us (43%)
  local copies, waits for them, and re-layouts  28 us (4%)
  other arithmetic  17.1 us (2%)
  between operations  14.8 us (2%)
    dot_general x17, matrix products, dot(): return lax.dot_general(a, b, (dims, ((), ())), preferred_element_type=F32)  366 us
    reduce_scatter x6, waiting for transfers between devices, scatter(): return lax.psum_scatter(g, 'dp', scatter_dimension=0, tiled=True)  194 us
    all_gather x6, waiting for transfers between devices, gather(): return lax.all_gather(w, 'dp', axis=0, tiled=True)  136 us
    unnamed x27, local copies, waits for them, and re-layouts  22 us
  transfers between devices with their start and end apart: 12, of which 9 were waited for; matrix products, arithmetic and copies ran while one was open for 45% of the time, Pallas kernels for 0%

profile of v1, /device:TPU:0, one launch (start us, length us, event | category | flops | bytes accessed | tf_op | source)
XLA Modules:
  0.0 757.1 jit_solution(5733012342861294334)
XLA Ops:
  7.2 2.0 fusion.64
  9.2 0.0 all-gather.17.cloned.1.call-start
  9.3 2.0 fusion.66
  11.3 0.0 all-gather.19.cloned.1.call-start
  11.4 2.0 fusion.65
  13.4 0.5 all-gather.13.cloned.1.call-update
  14.0 0.5 all-gather.21.cloned.1.call-update
  14.6 0.5 all-gather.23.cloned.1.call-update
  15.2 6.4 copy.10
  21.6 3.1 fusion.13
  24.7 0.6 copy-done.6
  25.3 28.5 %all-gather.15.cloned.1.call-done = bf16[1,1024,2816]{2,1,0:T(8,128)(2,1)} async-done(((bf16[1,64,2816]{2,1,0:T(8,128)(2,1)}), bf16[1,1024,2816]{2,1,0:T(8,128)(2,1)}) %all-gather.15.cloned.1.call-update) | async-done | bytes 5767184 | tf_op jit(solution)/shard_map/all_gather | solution.py:42
  53.8 19.9 %fusion.36 = f32[2048,2816]{1,0:T(8,128)} fusion(bf16[1,1024,2816]{2,1,0:T(8,128)(2,1)} %all-gather.15.cloned.1.call-done, bf16[1,2048,1024]{1,2,0:T(8,128)(2,1)} %copy.10, f32[2048]{0:T(1024)S(1)} %add_rsqrt_fusion.1), kind=kOutput, calls=%fused_computation.58 | convolution fusion | flops 11817451520 | bytes 33038336 | tf_op jit(solution)/shard_map/dot_general | solution.py:11
  73.7 22.5 %all-gather.17.cloned.1.call-done = bf16[1,1024,2816]{2,1,0:T(8,128)(2,1)} async-done(((bf16[1,64,2816]{2,1,0:T(8,128)(2,1)}), bf16[1,1024,2816]{2,1,0:T(8,128)(2,1)}) %all-gather.17.cloned.1.call-update) | async-done | bytes 5767184 | tf_op jit(solution)/shard_map/all_gather | solution.py:42
  96.2 27.8 %multiply_convert_fusion.1 = (bf16[2048,2816]{1,0:T(8,128)(2,1)}, f32[2048,2816]{1,0:T(8,128)}) fusion(f32[2048,2816]{1,0:T(8,128)} %fusion.36, bf16[1,1024,2816]{2,1,0:T(8,128)(2,1)} %all-gather.17.cloned.1.call-done, bf16[1,2048,1024]{1,2,0:T(8,128)(2,1)} %copy.10, f32[2048]{0:T(1024)S(1)} %add_rsqrt_fusion.1), kind=kOutput, calls=%fused_computation.14 | convolution fusion | flops 11852054528 | bytes 67641344 | tf_op jit(solution)/shard_map/dot_general | solution.py:11
  124.0 14.6 %all-gather.19.cloned.1.call-done = bf16[1,2816,1024]{2,1,0:T(8,128)(2,1)} async-done(((bf16[1,176,1024]{2,1,0:T(8,128)(2,1)}), bf16[1,2816,1024]{2,1,0:T(8,128)(2,1)}) %all-gather.19.cloned.1.call-update) | async-done | bytes 5767184 | tf_op jit(solution)/shard_map/all_gather | solution.py:42
  138.6 19.6 %fusion.16 = (f32[2048]{0:T(1024)S(1)}, bf16[2048,1024]{0,1:T(8,128)(2,1)}) fusion(bf16[2048,2816]{1,0:T(8,128)(2,1)} %get-tuple-element.18, bf16[1,2816,1024]{2,1,0:T(8,128)(2,1)} %all-gather.19.cloned.1.call-done, bf16[1,2048,1024]{1,2,0:T(8,128)(2,1)} %copy.10), kind=kOutput, calls=%fused_computation.36 | convolution fusion | flops 11821643776 | bytes 25698304 | tf_op jit(solution)/shard_map/dot_general | solution.py:11
  158.2 22.6 %all-gather.13.cloned.1.call-done = bf16[1,2816,1024]{2,1,0:T(8,128)(2,1)} async-done(((bf16[1,176,1024]{2,1,0:T(8,128)(2,1)}), bf16[1,2816,1024]{2,1,0:T(8,128)(2,1)}) %all-gather.13.cloned.1.call-update) | async-done | bytes 5767184 | tf_op jit(solution)/shard_map/all_gather | solution.py:42
  180.9 18.1 %convolution_convert_fusion.1 = bf16[2048,2816]{1,0:T(8,128)(2,1)} fusion(bf16[1,2816,1024]{2,1,0:T(8,128)(2,1)} %all-gather.13.cloned.1.call-done, bf16[1,2048,1024]{2,1,0:T(8,128)(2,1)} %param.6), kind=kOutput, calls=%fused_computation.26 | convolution fusion | flops 11816927232 | bytes 21495808 | tf_op jit(solution)/shard_map/dot_general | solution.py:11
  199.0 24.7 %all-gather.21.cloned.1.call-done = bf16[1,1024,2816]{2,1,0:T(8,128)(2,1)} async-done(((bf16[1,64,2816]{2,1,0:T(8,128)(2,1)}), bf16[1,1024,2816]{2,1,0:T(8,128)(2,1)}) %all-gather.21.cloned.1.call-update) | async-done | bytes 5767184 | tf_op jit(solution)/shard_map/all_gather | solution.py:42
  223.7 20.1 %fusion.25 = f32[2048,2816]{1,0:T(8,128)} fusion(bf16[1,1024,2816]{2,1,0:T(8,128)(2,1)} %all-gather.21.cloned.1.call-done, bf16[2048,1024]{0,1:T(8,128)(2,1)} %get-tuple-element.21, f32[2048]{0:T(1024)S(1)} %add_rsqrt_fusion), kind=kOutput, calls=%fused_computation.47 | convolution fusion | flops 11817451520 | bytes 33038336 | tf_op jit(solution)/shard_map/dot_general | solution.py:11
  243.8 22.7 %all-gather.23.cloned.1.call-done = bf16[1,1024,2816]{2,1,0:T(8,128)(2,1)} async-done(((bf16[1,64,2816]{2,1,0:T(8,128)(2,1)}), bf16[1,1024,2816]{2,1,0:T(8,128)(2,1)}) %all-gather.23.cloned.1.call-update) | async-done | bytes 5767184 | tf_op jit(solution)/shard_map/all_gather | solution.py:42
  266.5 37.3 %fusion.3 = (bf16[2048,2816]{1,0:T(8,128)(2,1)}, bf16[2048,2816]{1,0:T(8,128)(2,1)}, f32[2048,2816]{1,0:T(8,128)}) fusion(bf16[2048,2816]{1,0:T(8,128)(2,1)} %convolution_convert_fusion.1, f32[2048,2816]{1,0:T(8,128)} %fusion.25, bf16[1,1024,2816]{2,1,0:T(8,128)(2,1)} %all-gather.23.cloned.1.call-done, bf16[2048,1024]{0,1:T(8,128)(2,1)} %get-tuple-element.21, ...), kind=kOutput, calls=%fused_computation.7 | convolution fusion | flops 11898191872 | bytes 90710016 | tf_op jit(solution)/shard_map/dot_general | solution.py:11
  303.8 23.7 %fusion.39 = bf16[2816,1024]{1,0:T(8,128)(2,1)} fusion(f32[2048,2816]{1,0:T(8,128)} %fusion.25, f32[2048,2816]{1,0:T(8,128)} %get-tuple-element.22, bf16[1,2048,1024]{2,1,0:T(8,128)(2,1)S(1)} %copy-done.5), kind=kOutput, calls=%fused_computation.61 | convolution fusion | flops 11848646656 | bytes 56098816 | tf_op jit(solution)/shard_map/dot_general | solution.py:11
  327.6 0.0 reduce-scatter.15.cloned.1.call-start
  327.6 6.6 copy.9
  334.2 18.8 %fusion.19 = f32[2048,1024]{0,1:T(8,128)} fusion(bf16[2048,2816]{1,0:T(8,128)(2,1)} %get-tuple-element.11, bf16[1,1024,2816]{2,1,0:T(8,128)(2,1)} %all-gather.23.cloned.1.call-done), kind=kOutput, calls=%fused_computation.41 | convolution fusion | flops 11811160064 | bytes 25690112 | tf_op jit(solution)/shard_map/dot_general | solution.py:11
  353.0 18.1 %fusion.18 = (f32[2048]{0:T(1024)S(1)}, bf16[2048,1024]{0,1:T(8,128)(2,1)S(1)}) fusion(bf16[2048,1024]{0,1:T(8,128)(2,1)S(1)} %copy-done.4, f32[2048,1024]{0,1:T(8,128)} %fusion.19, bf16[2048,2816]{1,0:T(8,128)(2,1)} %get-tuple-element.10, bf16[1,1024,2816]{2,1,0:T(8,128)(2,1)} %all-gather.21.cloned.1.call-done), kind=kOutput, calls=%fused_computation.38 | convolution fusion | flops 11823740928 | bytes 34086912 | tf_op jit(solution)/shard_map/dot_general | solution.py:11
  371.2 3.2 fusion.42
  374.3 1.9 copy-done.1
  376.3 16.9 %convolution_convert_fusion.2 = bf16[2816,1024]{1,0:T(8,128)(2,1)} fusion(bf16[2048,2816]{1,0:T(8,128)(2,1)} %get-tuple-element.18, bf16[2048,1024]{0,1:T(8,128)(2,1)S(1)} %fusion.42), kind=kOutput, calls=%fused_computation.62 | convolution fusion | flops 11814043648 | bytes 21495808 | tf_op jit(solution)/shard_map/dot_general | solution.py:11
  393.2 0.0 reduce-scatter.13.cloned.1.call-start
  393.2 18.6 %convolution_convert_fusion.3 = bf16[1024,2816]{1,0:T(8,128)(2,1)} fusion(bf16[2048,2816]{1,0:T(8,128)(2,1)} %get-tuple-element.10, bf16[2048,1024]{0,1:T(8,128)(2,1)} %get-tuple-element.21, f32[2048]{0:T(1024)S(1)} %add_rsqrt_fusion), kind=kOutput, calls=%fused_computation.63 | convolution fusion | flops 11820335104 | bytes 21504000 | tf_op jit(solution)/shard_map/dot_general | solution.py:11
  411.9 33.8 %fusion.5 = (bf16[2048,2816]{1,0:T(8,128)(2,1)}, bf16[2048,2816]{1,0:T(8,128)(2,1)}) fusion(f32[2048,2816]{1,0:T(8,128)} %get-tuple-element.19, f32[2048,2816]{1,0:T(8,128)} %fusion.36, bf16[2048,1024]{0,1:T(8,128)(2,1)} %copy-done.1, bf16[1,2816,1024]{2,1,0:T(8,128)(2,1)} %all-gather.19.cloned.1.call-done), kind=kOutput, calls=%fused_computation.9 | convolution fusion | flops 11897667584 | bytes 79167488 | tf_op jit(solution)/shard_map/dot_general | solution.py:11
  445.7 18.6 %convolution_convert_fusion.4 = bf16[1024,2816]{1,0:T(8,128)(2,1)} fusion(bf16[2048,2816]{1,0:T(8,128)(2,1)} %get-tuple-element.9, bf16[1,2048,1024]{1,2,0:T(8,128)(2,1)} %copy.10, f32[2048]{0:T(1024)S(1)} %copy-done.9), kind=kOutput, calls=%fused_computation.64 | convolution fusion | flops 11820335104 | bytes 21504000 | tf_op jit(solution)/shard_map/dot_general | solution.py:11
  464.3 0.0 reduce-scatter.9.cloned.1.call-start
  464.4 18.7 %convolution_convert_fusion.5 = bf16[1024,2816]{1,0:T(8,128)(2,1)} fusion(bf16[2048,2816]{1,0:T(8,128)(2,1)} %get-tuple-element.11, bf16[2048,1024]{0,1:T(8,128)(2,1)} %get-tuple-element.21, f32[2048]{0:T(1024)S(1)} %add_rsqrt_fusion), kind=kOutput, calls=%fused_computation.65 | convolution fusion | flops 11820335104 | bytes 21504000 | tf_op jit(solution)/shard_map/dot_general | solution.py:11
  483.2 18.9 %convolution_convert_fusion.6 = bf16[1024,2816]{1,0:T(8,128)(2,1)} fusion(bf16[2048,2816]{1,0:T(8,128)(2,1)} %get-tuple-element.8, bf16[1,2048,1024]{1,2,0:T(8,128)(2,1)} %copy.10, f32[2048]{0:T(1024)S(1)} %copy-done.9), kind=kOutput, calls=%fused_computation.66 | convolution fusion | flops 11820335104 | bytes 21504000 | tf_op jit(solution)/shard_map/dot_general | solution.py:11
  502.1 18.8 %fusion.30 = f32[2048,1024]{0,1:T(8,128)} fusion(bf16[2048,2816]{1,0:T(8,128)(2,1)} %get-tuple-element.9, bf16[1,1024,2816]{2,1,0:T(8,128)(2,1)} %all-gather.17.cloned.1.call-done), kind=kOutput, calls=%fused_computation.52 | convolution fusion | flops 11811160064 | bytes 25690112 | tf_op jit(solution)/shard_map/dot_general | solution.py:11
  520.9 18.1 %fusion.15 = (f32[2048]{0:T(1024)S(1)}, bf16[2048,1024]{0,1:T(8,128)(2,1)S(1)}) fusion(bf16[1,2048,1024]{1,2,0:T(8,128)(2,1)S(1)} %copy-done, f32[2048,1024]{0,1:T(8,128)} %fusion.30, bf16[2048,2816]{1,0:T(8,128)(2,1)} %get-tuple-element.8, bf16[1,1024,2816]{2,1,0:T(8,128)(2,1)} %all-gather.15.cloned.1.call-done), kind=kOutput, calls=%fused_computation.35 | convolution fusion | flops 11823740928 | bytes 34086912 | tf_op jit(solution)/shard_map/dot_general | solution.py:11
  539.0 4.7 fusion.41
  543.8 6.4 copy.11
  550.2 2.0 pad_maximum_fusion.2
  552.2 55.9 %reduce-scatter.11.cloned.1.call-done = bf16[64,2816]{1,0:T(8,128)(2,1)} async-done(((bf16[1024,2816]{1,0:T(8,128)(2,1)}), bf16[64,2816]{1,0:T(8,128)(2,1)}) %reduce-scatter.11.cloned.1.call-update) | async-done | bytes 360464 | tf_op jit(solution)/shard_map/reduce_scatter | solution.py:46
  608.1 2.0 pad_maximum_fusion.1
  610.1 68.0 %reduce-scatter.9.cloned.1.call-done = bf16[64,2816]{1,0:T(8,128)(2,1)} async-done(((bf16[1024,2816]{1,0:T(8,128)(2,1)}), bf16[64,2816]{1,0:T(8,128)(2,1)}) %reduce-scatter.9.cloned.1.call-update) | async-done | bytes 360464 | tf_op jit(solution)/shard_map/reduce_scatter | solution.py:46
  678.1 69.6 %reduce-scatter.7.cloned.1.call-done = bf16[64,2816]{1,0:T(8,128)(2,1)} async-done(((bf16[1024,2816]{1,0:T(8,128)(2,1)}), bf16[64,2816]{1,0:T(8,128)(2,1)}) %reduce-scatter.7.cloned.1.call-update) | async-done | bytes 360464 | tf_op jit(solution)/shard_map/reduce_scatter | solution.py:46
  747.8 2.0 pad_maximum_fusion
  (45 shorter events, 0.5 us)
Async XLA Ops:
  7.2 46.6 %all-gather.15.cloned.1.call-start = ((), (), s32[]{:S(2)}) async-start(), calls=%async_computation.13 | async-start | bytes 6127616 | tf_op jit(solution)/shard_map/all_gather | solution.py:42
  9.2 87.0 %all-gather.17.cloned.1.call-start = ((), (), s32[]{:S(2)}) async-start(), calls=%async_computation.14 | async-start | bytes 6127616 | tf_op jit(solution)/shard_map/all_gather | solution.py:42
  11.3 127.3 %all-gather.19.cloned.1.call-start = ((), (), s32[]{:S(2)}) async-start(), calls=%async_computation.15 | async-start | bytes 6127616 | tf_op jit(solution)/shard_map/all_gather | solution.py:42
  13.4 167.5 %all-gather.13.cloned.1.call-start = ((), (), s32[]{:S(2)}) async-start(), calls=%async_computation.12 | async-start | bytes 6127616 | tf_op jit(solution)/shard_map/all_gather | solution.py:42
  14.0 209.7 %all-gather.21.cloned.1.call-start = ((), (), s32[]{:S(2)}) async-start(), calls=%async_computation.16 | async-start | bytes 6127616 | tf_op jit(solution)/shard_map/all_gather | solution.py:42
  14.6 252.0 %all-gather.23.cloned.1.call-start = ((), (), s32[]{:S(2)}) async-start(), calls=%async_computation.17 | async-start | bytes 6127616 | tf_op jit(solution)/shard_map/all_gather | solution.py:42
  15.1 535.0 %reduce-scatter.17.cloned.1.call-start = ((), (), s32[]{:S(2)}) async-start(), calls=%async_computation.11 | async-start | bytes 6127616 | tf_op jit(solution)/shard_map/reduce_scatter | solution.py:46
  24.7 0.6 copy-start.6
  25.3 70.9 %copy-start.8 = (f32[2048]{0:T(1024)}, f32[2048]{0:T(1024)S(1)}, u32[]{:S(2)}) copy-start(f32[2048]{0:T(1024)S(1)} %add_rsqrt_fusion.1) | copy-start | bytes 24580
  158.2 40.8 %copy-start.10 = (f32[2048]{0:T(1024)}, f32[2048]{0:T(1024)S(1)}, u32[]{:S(2)}) copy-start(f32[2048]{0:T(1024)S(1)} %get-tuple-element.20) | copy-start | bytes 24580
  266.5 37.3 %copy-start.5 = (bf16[1,2048,1024]{2,1,0:T(8,128)(2,1)S(1)}, bf16[1,2048,1024]{2,1,0:T(8,128)(2,1)}, u32[]{:S(2)}) copy-start(bf16[1,2048,1024]{2,1,0:T(8,128)(2,1)} %param.6) | copy-start | bytes 12582916
  327.6 222.6 %reduce-scatter.15.cloned.1.call-start = ((), (), s32[]{:S(2)}) async-start(), calls=%async_computation.10 | async-start | bytes 6127616 | tf_op jit(solution)/shard_map/reduce_scatter | solution.py:46
  334.2 18.8 %copy-start.4 = (bf16[2048,1024]{0,1:T(8,128)(2,1)S(1)}, bf16[2048,1024]{0,1:T(8,128)(2,1)}, u32[]{:S(2)}) copy-start(bf16[2048,1024]{0,1:T(8,128)(2,1)} %get-tuple-element.21) | copy-start | bytes 12582916
  353.0 18.1 %copy-start.11 = (f32[2048]{0:T(1024)S(1)}, f32[2048]{0:T(1024)}, u32[]{:S(2)}) copy-start(f32[2048]{0:T(1024)} %copy-done.10) | copy-start | bytes 24580
  353.0 18.2 %copy-start.3 = (bf16[1,2048,1024]{1,2,0:T(8,128)(2,1)S(1)}, bf16[1,2048,1024]{1,2,0:T(8,128)(2,1)}, u32[]{:S(2)}) copy-start(bf16[1,2048,1024]{1,2,0:T(8,128)(2,1)} %copy.9) | copy-start | bytes 12582916
  374.3 2.0 copy-start.1
  393.2 159.0 %reduce-scatter.13.cloned.1.call-start = ((), (), s32[]{:S(2)}) async-start(), calls=%async_computation.9 | async-start | bytes 6127616 | tf_op jit(solution)/shard_map/reduce_scatter | solution.py:46
  411.9 196.2 %reduce-scatter.11.cloned.1.call-start = ((), (), s32[]{:S(2)}) async-start(), calls=%async_computation.8 | async-start | bytes 6127616 | tf_op jit(solution)/shard_map/reduce_scatter | solution.py:46
  411.9 33.8 %copy-start.9 = (f32[2048]{0:T(1024)S(1)}, f32[2048]{0:T(1024)}, u32[]{:S(2)}) copy-start(f32[2048]{0:T(1024)} %copy-done.8) | copy-start | bytes 24580
  464.3 213.8 %reduce-scatter.9.cloned.1.call-start = ((), (), s32[]{:S(2)}) async-start(), calls=%async_computation.7 | async-start | bytes 6127616 | tf_op jit(solution)/shard_map/reduce_scatter | solution.py:46
  483.1 264.6 %reduce-scatter.7.cloned.1.call-start = ((), (), s32[]{:S(2)}) async-start(), calls=%async_computation.6 | async-start | bytes 6127616 | tf_op jit(solution)/shard_map/reduce_scatter | solution.py:46
  502.1 18.8 %copy-start = (bf16[1,2048,1024]{1,2,0:T(8,128)(2,1)S(1)}, bf16[1,2048,1024]{1,2,0:T(8,128)(2,1)}, u32[]{:S(2)}) copy-start(bf16[1,2048,1024]{1,2,0:T(8,128)(2,1)} %copy.10) | copy-start | bytes 12582916
  520.9 18.1 %copy-start.7 = (f32[2048]{0:T(1024)S(1)}, f32[2048]{0:T(1024)}, u32[]{:S(2)}) copy-start(f32[2048]{0:T(1024)} %copy-done.6) | copy-start | bytes 24580
  520.9 18.2 %copy-start.2 = (bf16[2048,1024]{0,1:T(8,128)(2,1)S(1)}, bf16[2048,1024]{0,1:T(8,128)(2,1)}, u32[]{:S(2)}) copy-start(bf16[2048,1024]{0,1:T(8,128)(2,1)} %copy-done.1) | copy-start | bytes 12582916
Sparse Core Ops, SparseCore 0:
  10.8 42.9 all-gather.14
  56.0 40.1 all-gather.16
  98.4 40.1 all-gather.18
  140.7 40.1 all-gather.12
  183.5 40.1 all-gather.20
  226.3 40.1 all-gather.22
  327.7 67.7 reduce-scatter.16
  397.7 69.5 reduce-scatter.14
  469.6 68.1 reduce-scatter.12
  540.0 68.0 reduce-scatter.10
  610.4 67.7 reduce-scatter.8
  680.3 67.4 reduce-scatter.6

commit v2 on v0

v2 whole, which is shorter than its diff:
```python
import functools

import jax
import jax.numpy as jnp
from jax import lax
from jax.experimental import pallas as pl
from jax.experimental.pallas import tpu as pltpu
from jax.sharding import PartitionSpec as P

F32, BF16 = jnp.float32, jnp.bfloat16
EPS = 1e-6
VMEM_LIMIT = 66_000_000
ANY = pl.BlockSpec(memory_space=pl.ANY)
BOTH = pl.ds(0, 2)
ORDERS = ((0, 1, 2), (1, 2, 0), (2, 0, 1))
PARTS = {2816: ((0, 1024), (1024, 896), (1920, 896)), 1024: ((0, 384), (384, 384), (768, 256))}
NN, NT, TN = ((1,), (0,)), ((1,), (1,)), ((0,), (0,))


def dot(a, b, dims=NN):
    return lax.dot_general(a, b, (dims, ((), ())), preferred_element_type=F32)


def place():
    i = lax.axis_index("dp")
    return [(i // 8) % 2, (i // 4) % 2, (i // 2) % 2, i % 2]


def peer(axis):
    i, step = lax.axis_index("dp"), 8 >> axis
    return {"dp": i + step * (1 - 2 * ((i // step) % 2))}


def remote(src, dst, send, recv, axis):
    return pltpu.make_async_remote_copy(
        src_ref=src, dst_ref=dst, send_sem=send, recv_sem=recv, device_id=peer(axis), device_id_type=pl.DeviceIdType.MESH
    )


def meet():
    barrier = pltpu.get_barrier_semaphore()
    for axis in range(4):
        pl.semaphore_signal(barrier, inc=1, device_id=peer(axis), device_id_type=pl.DeviceIdType.MESH)
    pl.semaphore_wait(barrier, 4)


class Gather:
    def __init__(self, layer, *blocks):
        n = self.n = len(blocks)
        self.layer, self.inputs = layer, blocks
        shapes = [b.shape[1:] for b in blocks]
        self.cols = [PARTS[s[1]] for s in shapes]
        self.out_shapes = [jax.ShapeDtypeStruct((2, 2, 2, 2, *s), BF16) for s in shapes]
        dma = pltpu.SemaphoreType.DMA
        self.scratch = [pltpu.VMEM(s, BF16) for s in shapes] + [dma((n, 2)), dma((n, 3, 4)), dma((n, 3, 4))]

    def events(self, blocks, wholes, scratch):
        own, (local, send, recv) = scratch[: self.n], scratch[self.n :]
        at = place()
        weights = range(self.n)

        def copy(w, p, stage):
            order, (start, size) = (*ORDERS[p], 3), self.cols[w][p]
            index = tuple(BOTH if a in order[:stage] else at[a] for a in range(4))
            columns = (slice(None), pl.ds(start, size))
            dst = wholes[w].at[(*index, *columns)]
            src = blocks[w].at[(self.layer, *columns)] if stage == 0 else dst
            return remote(src, dst, send.at[w, p, stage], recv.at[w, p, stage], order[stage])

        def take(w):
            return pltpu.make_async_copy(blocks[w].at[self.layer], own[w], local.at[w, 0])

        def put(w):
            return pltpu.make_async_copy(own[w], wholes[w].at[tuple(at)], local.at[w, 1])

        def first():
            for w in weights:
                take(w).start()
                for p in range(3):
                    copy(w, p, 0).start()
            for w in weights:
                take(w).wait()
                put(w).start()

        def later(w, stage):
            if stage == 1:
                put(w).wait()
            for p in range(3):
                copy(w, p, stage - 1).wait_recv()
                copy(w, p, stage).start()

        def last():
            for w in weights:
                for p in range(3):
                    copy(w, p, 3).wait_recv()
                    for stage in range(4):
                        copy(w, p, stage).wait_send()

        middle = [functools.partial(later, w, stage) for stage in (1, 2, 3) for w in weights]
        return [first, *middle, last]


class Scatter:
    def __init__(self, *terms):
        n = self.n = len(terms)
        self.inputs = terms
        shapes = [t.shape[4:] for t in terms]
        self.cols = [PARTS[s[1]] for s in shapes]
        self.rows = [s[0] for s in shapes]
        self.out_shapes = [jax.ShapeDtypeStruct(s, BF16) for s in shapes]
        dma = pltpu.SemaphoreType.DMA
        self.scratch = []
        for s in shapes:
            self.scratch += [pltpu.VMEM((*(2,) * lead, *s), BF16) for lead in (3, 3, 2, 1, 0)]
        self.scratch += [dma((n, 2)), dma((n, 2)), dma((n, 3, 3)), dma((n, 3, 3))]

    def events(self, terms, sums, scratch):
        held = [scratch[5 * w : 5 * w + 5] for w in range(self.n)]
        local, core, send, recv = scratch[5 * self.n :]
        at = place()
        cube = at[:3]
        items = [(w, p) for w in range(self.n) for p in range(3)]

        def swap(w):
            return remote(terms[w].at[BOTH, BOTH, BOTH, 1 - at[3]], held[w][1], core.at[w, 0], core.at[w, 1], 3)

        def take(w):
            return pltpu.make_async_copy(terms[w].at[BOTH, BOTH, BOTH, at[3]], held[w][0], local.at[w, 0])

        def put(w):
            return pltpu.make_async_copy(held[w][0].at[tuple(cube)], sums[w], local.at[w, 1])

        def columns(w, p):
            return pl.ds(*self.cols[w][p])

        def copy(w, p, stage):
            order = ORDERS[p]
            index = list(cube)
            index[order[stage]] = 1 - cube[order[stage]]
            for a in order[stage + 1 :]:
                index[a] = BOTH
            src = held[w][0].at[(*index, slice(None), columns(w, p))]
            dst = held[w][2 + stage].at[(*(BOTH,) * (2 - stage), slice(None), columns(w, p))]
            return remote(src, dst, send.at[w, p, stage], recv.at[w, p, stage], order[stage])

        def add(w, p, stage):
            order = ORDERS[p]
            free = order[stage + 1 :] if stage < 3 else ()
            chunk = 32 if self.rows[w] % 32 == 0 else 16
            for number in range(2 ** len(free)):
                index = list(cube)
                if stage < 3:
                    index[order[stage]] = 1 - cube[order[stage]]
                for k, a in enumerate(free):
                    index[a] = (number >> k) & 1

                def some_rows(i, index=index):
                    where = (pl.ds(pl.multiple_of(i * chunk, chunk), chunk), columns(w, p))
                    total = held[w][0][(*index, *where)].astype(F32) + held[w][1][(*index, *where)].astype(F32)
                    for j in range(stage):
                        rest = [index[a] for a in range(3) if a not in order[: j + 1]]
                        total += held[w][2 + j][(*rest, *where)].astype(F32)
                    held[w][0][(*index, *where)] = total.astype(BF16)

                pl.loop(0, self.rows[w] // chunk)(some_rows)

        def first():
            for w in range(self.n):
                swap(w).start()
                take(w).start()

        def leave(w, stage):
            if stage == 0:
                take(w).wait()
                swap(w).wait_recv()
            for p in range(3):
                if stage > 0:
                    copy(w, p, stage - 1).wait_recv()
                add(w, p, stage)
                if stage < 3:
                    copy(w, p, stage).start()
            if stage == 3:
                put(w).start()

        def last():
            for w in range(self.n):
                swap(w).wait_send()
                for p in range(3):
                    for stage in range(3):
                        copy(w, p, stage).wait_send()
                put(w).wait()

        middle = [functools.partial(leave, w, stage) for stage in range(4) for w in range(self.n)]
        return [first, *middle, last]


def call(name, body, steps, inputs, in_specs, out_shapes, out_specs, flops=0, scratch=(), side=None, when=(), number=None):
    n_in, n_out, n_scratch = len(inputs), len(out_shapes), len(scratch)
    s_in, s_out = (len(side.inputs), len(side.out_shapes)) if side else (0, 0)

    def kernel(*refs):
        ins, refs = refs[:n_in], refs[n_in:]
        side_ins, refs = refs[:s_in], refs[s_in:]
        outs, refs = refs[:n_out], refs[n_out:]
        side_outs, refs = refs[:s_out], refs[s_out:]
        own, side_scratch = refs[:n_scratch], refs[n_scratch:]
        step = pl.program_id(0)
        events = side.events(side_ins, side_outs, side_scratch) if side else []
        for k, event in enumerate(events):
            if k < len(when):

                def now(event=event, k=k):
                    if k == 0:
                        meet()
                    event()

                pl.when(step == when[k])(now)
        body(*ins, *outs, *own)
        if len(events) > len(when):

            def end():
                for event in events[len(when) :]:
                    event()

            pl.when(step == steps - 1)(end)

    params = dict(vmem_limit_bytes=VMEM_LIMIT, dimension_semantics=("arbitrary",))
    if side:
        params |= dict(collective_id=number, has_side_effects=True)
    return pl.pallas_call(
        kernel,
        name=name,
        grid=(steps,),
        in_specs=[*in_specs, *[ANY] * s_in],
        out_specs=[*out_specs, *[ANY] * s_out],
        out_shape=[*out_shapes, *(side.out_shapes if side else ())],
        scratch_shapes=[*scratch, *(side.scratch if side else ())],
        compiler_params=pltpu.CompilerParams(**params),
        cost_estimate=pl.CostEstimate(flops=flops, bytes_accessed=0, transcendentals=0),
    )(*inputs, *(side.inputs if side else ()))


def shape(*dims, dtype=BF16):
    return jax.ShapeDtypeStruct(dims, dtype)


def kept(*dims):
    return pl.BlockSpec(dims, lambda i: (0,) * len(dims), pipeline_mode=pl.Buffered(1))


def across(rows, size):
    return pl.BlockSpec((rows, size), lambda i: (0, i))


def down(size, cols):
    return pl.BlockSpec((size, cols), lambda i: (i, 0))


T, D, FF = 2048, 1024, 2816
MM = 2 * T * D * FF


def scale_of(wide):
    return lax.rsqrt(jnp.mean(wide**2, -1, keepdims=True) + EPS)


def normed(wide):
    return (wide * scale_of(wide)).astype(BF16)


def norm_body(x, a, at):
    wide = x[...].astype(F32)
    y = wide * scale_of(wide)
    a[...] = y.astype(BF16)
    at[...] = y.T.astype(BF16)


def norm(x, **side):
    n = 256
    return call("norm", norm_body, T // n, [x], [down(n, D)], [shape(T, D), shape(D, T)], [down(n, D), across(D, n)], **side)


def chunks(n=512):
    return [pl.ds(r, n) for r in range(0, T, n)]


def gate_up_body(a, wg, wu, gate, up, hid):
    for r in chunks():
        g, u = dot(a[r, :], wg[...]), dot(a[r, :], wu[...])
        gate[r, :], up[r, :] = g, u
        hid[r, :] = (g * jax.nn.sigmoid(g) * u).astype(BF16)


def gate_up(a, wg, wu, **side):
    n = 256
    wide = shape(T, FF, dtype=F32)
    return call(
        "gate_up", gate_up_body, FF // n, [a, wg, wu], [kept(T, D), across(D, n), across(D, n)],
        [wide, wide, shape(T, FF)], [across(T, n)] * 3, flops=2 * MM, **side,
    )


def down_body(hid, wd, x, h, a, at):
    y = x[...] + dot(hid[...], wd[...]).astype(BF16)
    h[...] = y
    wide = y.astype(F32)
    y = wide * scale_of(wide)
    a[...] = y.astype(BF16)
    at[...] = y.T.astype(BF16)


def down_norm(hid, wd, x, **side):
    n = 256
    return call(
        "down", down_body, T // n, [hid, wd, x], [down(n, FF), kept(FF, D), down(n, D)],
        [shape(T, D), shape(T, D), shape(D, T)], [down(n, D), down(n, D), across(D, n)], flops=MM, **side,
    )


def gated_back(g, u, d):
    s = jax.nn.sigmoid(g)
    gs = g * s
    return (d * u * (s + gs * (1 - s))).astype(BF16), (d * gs).astype(BF16), (gs * u).astype(BF16)


def turn_body(a, dy, wg, wu, wd, hid, dgate, dup):
    for r in chunks(256):
        g, u = dot(a[r, :], wg[...]), dot(a[r, :], wu[...])
        d = dot(dy[r, :], wd[...], NT).astype(BF16).astype(F32)
        dgate[r, :], dup[r, :], hid[r, :] = gated_back(g, u, d)


def turn(a, dy, wg, wu, wd, **side):
    n = 256
    return call(
        "turn", turn_body, FF // n, [a, dy, wg, wu, wd],
        [kept(T, D), kept(T, D), across(D, n), across(D, n), down(n, D)],
        [shape(T, FF)] * 3, [across(T, n)] * 3, flops=3 * MM, **side,
    )


def hidden_back_body(dh, wd, gate, up, dgate, dup):
    for r in chunks(256):
        d = dot(dh[r, :], wd[...], NT).astype(BF16).astype(F32)
        dgate[r, :], dup[r, :], _ = gated_back(gate[r, :], up[r, :], d)


def hidden_back(dh, wd, gate, up, **side):
    n = 256
    return call(
        "hidden_back", hidden_back_body, FF // n, [dh, wd, gate, up],
        [kept(T, D), down(n, D), across(T, n), across(T, n)], [shape(T, FF)] * 2, [across(T, n)] * 2, flops=MM, **side,
    )


def grad_down_body(hid, dy, out):
    out[...] = dot(hid[...], dy[...], TN).astype(BF16)


def grad_down(hid, dy, **side):
    n = 256
    return call("grad_down", grad_down_body, FF // n, [hid, dy], [across(T, n), kept(T, D)], [shape(FF, D)], [down(n, D)], flops=MM, **side)


def grad_in_body(at, d, out):
    out[...] = dot(at[...], d[...]).astype(BF16)


def grad_in(at, d, **side):
    n = 256
    return call("grad_in", grad_in_body, FF // n, [at, d], [kept(D, T), across(T, n)], [shape(D, FF)], [across(D, n)], flops=MM, **side)


def back_body(dg, du, wg, wu, h, dy, out):
    da = (dot(dg[...], wg[...], NT) + dot(du[...], wu[...], NT)).astype(BF16).astype(F32)
    wide = h[...].astype(F32)
    s = scale_of(wide)
    through = jnp.sum(da * wide, -1, keepdims=True)
    out[...] = dy[...] + (da * s - wide * (s * s * s * through / D)).astype(BF16)


def back(dg, du, wg, wu, h, dy, **side):
    n = 256
    return call(
        "back", back_body, T // n, [dg, du, wg, wu, h, dy],
        [down(n, FF), down(n, FF), kept(D, FF), kept(D, FF), down(n, D), down(n, D)],
        [shape(T, D)], [down(n, D)], flops=2 * MM, **side,
    )


def blocks_of(grad):
    return grad.reshape(2, 2, 2, 2, -1, grad.shape[-1])


def device_step(x, dy, w_gate, w_up, w_down):
    x, dy = x.reshape(T, D), dy.reshape(T, D)

    a0, a0t, wg0, wu0, wd0 = norm(x, side=Gather(0, w_gate, w_up, w_down), when=(0, 2, 3, 4), number=1)
    wg0, wu0, wd0 = wg0.reshape(D, FF), wu0.reshape(D, FF), wd0.reshape(FF, D)
    gate0, up0, hid0, wg1, wu1 = gate_up(a0, wg0, wu0, side=Gather(1, w_gate, w_up), when=(0, 1, 2, 4, 6, 10), number=2)
    h1, a1, a1t, wd1 = down_norm(hid0, wd0, x, side=Gather(1, w_down), when=(0, 2, 4), number=3)
    wg1, wu1, wd1 = wg1.reshape(D, FF), wu1.reshape(D, FF), wd1.reshape(FF, D)

    hid1, dgate1, dup1 = turn(a1, dy, wg1, wu1, wd1)
    (gd1,) = grad_down(hid1, dy)
    gg1, sd1 = grad_in(a1t, dgate1, side=Scatter(blocks_of(gd1)), when=(0, 4), number=4)
    (gu1,) = grad_in(a1t, dup1)
    dh1, sg1, su1 = back(dgate1, dup1, wg1, wu1, h1, dy, side=Scatter(blocks_of(gg1), blocks_of(gu1)), when=(0, 2, 3, 5, 7), number=5)

    (gd0,) = grad_down(hid0, dh1)
    dgate0, dup0, sd0 = hidden_back(dh1, wd0, gate0, up0, side=Scatter(blocks_of(gd0)), when=(0, 3, 6, 9), number=6)
    (gg0,) = grad_in(a0t, dgate0)
    gu0, sg0 = grad_in(a0t, dup0, side=Scatter(blocks_of(gg0)), when=(0, 4), number=7)
    dx, su0 = back(dgate0, dup0, wg0, wu0, x, dh1, side=Scatter(blocks_of(gu0)), when=(0, 2, 5, 7), number=8)
    return dx[None], jnp.stack([sg0, sg1]), jnp.stack([su0, su1]), jnp.stack([sd0, sd1])


def solution(mesh):
    tokens, rows = P(("rep", "dp"), None, None), P(None, "dp", None)
    return jax.shard_map(
        device_step,
        mesh=mesh,
        in_specs=(tokens, tokens, rows, rows, rows),
        out_specs=(tokens, P("rep", "dp", None), P("rep", "dp", None), P("rep", "dp", None)),
        check_vma=False,
    )
```

time: 1510 us -> 497 us (0.33)
  Pallas kernels: 0 us -> 485 us
  starting transfers between devices: 466 us -> 0 us
  matrix products: 444 us -> 0 us
  waiting for transfers between devices: 292 us -> 0 us
  other arithmetic: 183 us -> 4.23 us
  local copies, waits for them, and re-layouts: 99.6 us -> 4.65 us
    pallas_call x0 -> x13, Pallas kernels: none -> 485 us  [call(): pl.pallas_call(kernel, name=name, grid=(steps,), in_specs=[*in_specs, *[A...]
    dot_general x119 -> x0, starting transfers between devices: 466 us -> none  [the longest x51 185 us: matmul(): jnp.dot(a, w, preferred_element_type=jnp.float32).astype(jnp.bfloat16)]
    dot_general x66 -> x0, matrix products: 444 us -> none  [the longest x26 153 us: matmul(): jnp.dot(a, w, preferred_element_type=jnp.float32).astype(jnp.bfloat16)]
    dot_general x119 -> x0, waiting for transfers between devices: 291 us -> none  [the longest x51 127 us: matmul(): jnp.dot(a, w, preferred_element_type=jnp.float32).astype(jnp.bfloat16)]
    dot_general x112 -> x0, other arithmetic: 126 us -> none
    unnamed x54 -> x7, local copies, waits for them, and re-layouts: 57.6 us -> 4.65 us
    dot_general x146 -> x0, local copies, waits for them, and re-layouts: 36.1 us -> none  [the longest x18 35.9 us: matmul(): jnp.dot(a, w, preferred_element_type=jnp.float32).astype(jnp.bfloat16)]
    mul x3 -> x0, other arithmetic: 20.5 us -> none  [the longest x1 20.4 us: layer(): jax.nn.silu(gate) * up]
  transfers between devices with their start and end apart: 124 -> 0, of which waited for: 91 -> 0; matrix products, arithmetic and copies ran while one was open for 45% -> 0% of each run, Pallas kernels for 0% -> 0%
where the time goes in v2:
time: 497 us; the launch traced here: 495 us
  Pallas kernels  485 us (98%)
    pallas_call x13, Pallas kernels, call(): pl.pallas_call(kernel, name=name, grid=(steps,), in_specs=[*in_specs, *[A...  485 us

profile of v2, /device:TPU:0, one launch (start us, length us, event | category | flops | bytes accessed | tf_op | source)
XLA Modules:
  0.0 495.1 jit_solution(4682555092864101097)
XLA Ops:
  0.6 69.4 %norm.1 = (bf16[2048,1024]{1,0:T(8,128)(2,1)}, bf16[1024,2048]{1,0:T(8,128)(2,1)}, bf16[2,2,2,2,64,2816]{5,4,3,2,1,0:T(8,128)(2,1)}, bf16[2,2,2,2,64,2816]{5,4,3...) custom-call(bf16[2048,1024]{1,0:T(8,128)(2,1)} %bitcast.24, bf16[2,64,2816]{2,1,0:T(8,128)(2,1)} %refs_3_.4, ...), custom_call_target="tpu_custom_call" | custom-call | tf_op jit(solution)/shard_map/norm/pallas_call | solution.py:230
  70.1 50.5 %gate_up.1 = (f32[2048,2816]{1,0:T(8,128)}, f32[2048,2816]{1,0:T(8,128)}, bf16[2048,2816]{1,0:T(8,128)(2,1)}, bf16[2,2,2,2,64,2816]{5,4,3,2,1,0:T(8,128)(2,1)}, bf16[2,2,2,2,64,2816]{5,4,3,2,1,0:T(8,128)(2,1)}) custom-call(bf16[2048,1024]{1,0:T(8,128)(2,1)} %get-tuple-element.33.refs_0_, bf16[1024,2816]{1,0:T(8,128)(2,1)} %bitcast.34, ...), custom_call_target="tpu_custom_call" | custom-call | flops 23622320128 | tf_op jit(solution)/shard_map/gate_up/pallas_call | solution.py:230
  120.6 36.9 %down.1 = (bf16[2048,1024]{1,0:T(8,128)(2,1)}, bf16[2048,1024]{1,0:T(8,128)(2,1)}, bf16[1024,2048]{1,0:T(8,128)(2,1)}, bf16[2,2,2,2,176,1024]{5,4,3,2,1,0:T(8,128)(2,1)}) custom-call(bf16[2048,2816]{1,0:T(8,128)(2,1)} %get-tuple-element.36.refs_0_, bf16[2816,1024]{1,0:T(8,128)(2,1)} %bitcast.21, bf16[2048,1024]{1,0:T(8,128)(2,1)} %bitcast.25, ...), custom_call_target="tpu_custom_call" | custom-call | flops 11811160064 | tf_op jit(solution)/shard_map/down/pallas_call | solution.py:230
  157.6 45.8 %turn.1 = (bf16[2048,2816]{1,0:T(8,128)(2,1)}, bf16[2048,2816]{1,0:T(8,128)(2,1)}, bf16[2048,2816]{1,0:T(8,128)(2,1)}) custom-call(bf16[2048,1024]{1,0:T(8,128)(2,1)} %get-tuple-element.38.refs_0_, bf16[2048,1024]{1,0:T(8,128)(2,1)} %bitcast.38, bf16[1024,2816]{1,0:T(8,128)(2,1)} %bitcast.41, bf16[1024,2816]{1,0:T(8,128)(2,1)} %bitcast.43, ...), custom_call_target="tpu_custom_call" | custom-call | flops 35433480192 | tf_op jit(solution)/shard_map/turn/pallas_call | solution.py:230
  203.3 18.2 %grad_down.2 = bf16[2816,1024]{1,0:T(8,128)(2,1)} custom-call(bf16[2048,2816]{1,0:T(8,128)(2,1)} %get-tuple-element.46.refs_0_, bf16[2048,1024]{1,0:T(8,128)(2,1)} %bitcast.39), custom_call_target="tpu_custom_call" | custom-call | flops 11811160064 | tf_op jit(solution)/shard_map/grad_down/pallas_call | solution.py:230
  221.5 36.9 %grad_in.4 = (bf16[1024,2816]{1,0:T(8,128)(2,1)}, bf16[176,1024]{1,0:T(8,128)(2,1)}) custom-call(bf16[1024,2048]{1,0:T(8,128)(2,1)} %get-tuple-element.45.refs_0_, bf16[2048,2816]{1,0:T(8,128)(2,1)} %get-tuple-element.42.refs_1_.refs_0_, bf16[2,2,2,2,176,1024]{5,4,3,2,1,0:T(8,128)(2,1)} %bitcast.49), custom_call_target="tpu_custom_call" | custom-call | flops 11811160064 | tf_op jit(solution)/shard_map/grad_in/pallas_call | solution.py:230
  258.4 18.1 %grad_in.5 = bf16[1024,2816]{1,0:T(8,128)(2,1)} custom-call(bf16[1024,2048]{1,0:T(8,128)(2,1)} %get-tuple-element.45.refs_0_, bf16[2048,2816]{1,0:T(8,128)(2,1)} %get-tuple-element.43.refs_1_), custom_call_target="tpu_custom_call" | custom-call | flops 11811160064 | tf_op jit(solution)/shard_map/grad_in/pallas_call | solution.py:230
  276.5 55.0 %back.2 = (bf16[2048,1024]{1,0:T(8,128)(2,1)}, bf16[64,2816]{1,0:T(8,128)(2,1)}, bf16[64,2816]{1,0:T(8,128)(2,1)}) custom-call(bf16[2048,2816]{1,0:T(8,128)(2,1)} %get-tuple-element.42.refs_1_.refs_0_, bf16[2048,2816]{1,0:T(8,128)(2,1)} %get-tuple-element.43.refs_1_, bf16[1024,2816]{1,0:T(8,128)(2,1)} %bitcast.42, bf16[1024,2816]{1,0:T(8,128)(2,1)} %bitcast.44, ...), custom_call_target="tpu_custom_call" | custom-call | flops 23622320128 | tf_op jit(solution)/shard_map/back/pallas_call | solution.py:230
  331.5 18.2 %grad_down.3 = bf16[2816,1024]{1,0:T(8,128)(2,1)} custom-call(bf16[2048,2816]{1,0:T(8,128)(2,1)} %get-tuple-element.36.refs_0_, bf16[2048,1024]{1,0:T(8,128)(2,1)} %get-tuple-element.48.refs_1_.refs_0_.refs_5_), custom_call_target="tpu_custom_call" | custom-call | flops 11811160064 | tf_op jit(solution)/shard_map/grad_down/pallas_call | solution.py:230
  349.7 0.0 copy-start.2
  349.7 42.8 %hidden_back.1 = (bf16[2048,2816]{1,0:T(8,128)(2,1)}, bf16[2048,2816]{1,0:T(8,128)(2,1)}, bf16[176,1024]{1,0:T(8,128)(2,1)}) custom-call(bf16[2048,1024]{1,0:T(8,128)(2,1)} %get-tuple-element.48.refs_1_.refs_0_.refs_5_, bf16[2816,1024]{1,0:T(8,128)(2,1)} %bitcast.22, f32[2048,2816]{1,0:T(8,128)} %get-tuple-element.49.refs_2_, ...), custom_call_target="tpu_custom_call" | custom-call | flops 11811160064 | tf_op jit(solution)/shard_map/hidden_back/pallas_call | solution.py:230
  392.6 0.0 copy-done.2
  392.6 1.9 pad_maximum_fusion.2
  394.5 18.1 %grad_in.6 = bf16[1024,2816]{1,0:T(8,128)(2,1)} custom-call(bf16[1024,2048]{1,0:T(8,128)(2,1)} %get-tuple-element.53.refs_0_, bf16[2048,2816]{1,0:T(8,128)(2,1)} %get-tuple-element.51.refs_1_.refs_0_), custom_call_target="tpu_custom_call" | custom-call | flops 11811160064 | tf_op jit(solution)/shard_map/grad_in/pallas_call | solution.py:230
  412.6 35.0 %grad_in.7 = (bf16[1024,2816]{1,0:T(8,128)(2,1)}, bf16[64,2816]{1,0:T(8,128)(2,1)}) custom-call(bf16[1024,2048]{1,0:T(8,128)(2,1)} %get-tuple-element.53.refs_0_, bf16[2048,2816]{1,0:T(8,128)(2,1)} %get-tuple-element.52.refs_1_, bf16[2,2,2,2,64,2816]{5,4,3,2,1,0:T(8,128)(2,1)} %bitcast.50), custom_call_target="tpu_custom_call" | custom-call | flops 11811160064 | tf_op jit(solution)/shard_map/grad_in/pallas_call | solution.py:230
  447.7 0.0 copy-start
  447.7 0.0 copy-start.1
  447.7 40.4 %back.3 = (bf16[2048,1024]{1,0:T(8,128)(2,1)}, bf16[64,2816]{1,0:T(8,128)(2,1)}) custom-call(bf16[2048,2816]{1,0:T(8,128)(2,1)} %get-tuple-element.51.refs_1_.refs_0_, bf16[2048,2816]{1,0:T(8,128)(2,1)} %get-tuple-element.52.refs_1_, bf16[1024,2816]{1,0:T(8,128)(2,1)} %bitcast.35, bf16[1024,2816]{1,0:T(8,128)(2,1)} %bitcast.37, bf16[2048,1024]{1,0:T(8,128)(2,1)} %bitcast.26, ...), custom_call_target="tpu_custom_call" | custom-call | flops 23622320128 | tf_op jit(solution)/shard_map/back/pallas_call | solution.py:230
  488.1 0.0 copy-done
  488.1 0.0 copy-done.1
  488.1 2.3 pad_maximum_fusion
  490.5 4.6 copy.10
Async XLA Ops:
  349.7 42.8 %copy-start.2 = (bf16[176,1024]{1,0:T(8,128)(2,1)S(1)}, bf16[176,1024]{1,0:T(8,128)(2,1)}, u32[]{:S(2)}) copy-start(bf16[176,1024]{1,0:T(8,128)(2,1)} %get-tuple-element.61) | copy-start | bytes 1081348
  447.7 40.5 %copy-start = (bf16[64,2816]{1,0:T(8,128)(2,1)S(1)}, bf16[64,2816]{1,0:T(8,128)(2,1)}, u32[]{:S(2)}) copy-start(bf16[64,2816]{1,0:T(8,128)(2,1)} %get-tuple-element.57) | copy-start | bytes 1081348
  447.7 40.5 %copy-start.1 = (bf16[64,2816]{1,0:T(8,128)(2,1)S(1)}, bf16[64,2816]{1,0:T(8,128)(2,1)}, u32[]{:S(2)}) copy-start(bf16[64,2816]{1,0:T(8,128)(2,1)} %get-tuple-element.59) | copy-start | bytes 1081348

commit v3 on v2

--- a/solution.py
+++ b/solution.py
@@ -13,7 +13,12 @@
 ANY = pl.BlockSpec(memory_space=pl.ANY)
 BOTH = pl.ds(0, 2)
 ORDERS = ((0, 1, 2), (1, 2, 0), (2, 0, 1))
-PARTS = {2816: ((0, 1024), (1024, 896), (1920, 896)), 1024: ((0, 384), (384, 384), (768, 256))}
+PARTS = {
+    2816: ((0, 1024), (1024, 896), (1920, 896)),
+    1536: ((0, 512), (512, 512), (1024, 512)),
+    1280: ((0, 512), (512, 384), (896, 384)),
+    1024: ((0, 384), (384, 384), (768, 256)),
+}
 NN, NT, TN = ((1,), (0,)), ((1,), (1,)), ((0,), (0,))
 
 
@@ -45,30 +50,45 @@
 
 
 class Gather:
-    def __init__(self, layer, *blocks):
-        n = self.n = len(blocks)
-        self.layer, self.inputs = layer, blocks
-        shapes = [b.shape[1:] for b in blocks]
-        self.cols = [PARTS[s[1]] for s in shapes]
+    def __init__(self, *weights):
+        n = self.n = len(weights)
+        self.inputs, self.layers, self.starts, sizes, self.shifts = zip(*weights)
+        shapes = [(b.shape[1], size) for b, size in zip(self.inputs, sizes)]
+        self.cols = [PARTS[size] for size in sizes]
         self.out_shapes = [jax.ShapeDtypeStruct((2, 2, 2, 2, *s), BF16) for s in shapes]
         dma = pltpu.SemaphoreType.DMA
-        self.scratch = [pltpu.VMEM(s, BF16) for s in shapes] + [dma((n, 2)), dma((n, 3, 4)), dma((n, 3, 4))]
+        self.scratch = [pltpu.VMEM(s, BF16) for s in shapes] + [dma((n, 2)), *[dma((n, 3, k)) for k in (3, 3, 4, 4)]]
 
     def events(self, blocks, wholes, scratch):
-        own, (local, send, recv) = scratch[: self.n], scratch[self.n :]
+        own, (local, send, recv, relay_send, relay_recv) = scratch[: self.n], scratch[self.n :]
         at = place()
         weights = range(self.n)
 
+        def part(w, p, index):
+            start, size = self.cols[w][p]
+            return wholes[w].at[(*index, slice(None), pl.ds(start, size))]
+
+        def block(w, p):
+            start, size = self.cols[w][p]
+            return blocks[w].at[(self.layers[w], slice(None), pl.ds(self.starts[w] + start, size))]
+
         def copy(w, p, stage):
-            order, (start, size) = (*ORDERS[p], 3), self.cols[w][p]
-            index = tuple(BOTH if a in order[:stage] else at[a] for a in range(4))
-            columns = (slice(None), pl.ds(start, size))
-            dst = wholes[w].at[(*index, *columns)]
-            src = blocks[w].at[(self.layer, *columns)] if stage == 0 else dst
-            return remote(src, dst, send.at[w, p, stage], recv.at[w, p, stage], order[stage])
+            order = ORDERS[(p + self.shifts[w]) % 3]
+            dst = part(w, p, [BOTH if a in order[:stage] else at[a] for a in range(4)])
+            return remote(dst if stage else block(w, p), dst, send.at[w, p, stage], recv.at[w, p, stage], order[stage])
+
+        def relay(w, p, stage):
+            index, order = list(at), ORDERS[(p + self.shifts[w]) % 3]
+            if stage:
+                index[order[stage - 1]] = 1 - at[order[stage - 1]]
+                for a in order[: stage - 1]:
+                    index[a] = BOTH
+            dst = part(w, p, index)
+            return remote(dst if stage else block(w, p), dst, relay_send.at[w, p, stage], relay_recv.at[w, p, stage], 3)
 
         def take(w):
-            return pltpu.make_async_copy(blocks[w].at[self.layer], own[w], local.at[w, 0])
+            block = blocks[w].at[(self.layers[w], slice(None), pl.ds(self.starts[w], own[w].shape[1]))]
+            return pltpu.make_async_copy(block, own[w], local.at[w, 0])
 
         def put(w):
             return pltpu.make_async_copy(own[w], wholes[w].at[tuple(at)], local.at[w, 1])
@@ -79,6 +99,8 @@
                 for p in range(3):
                     copy(w, p, 0).start()
             for w in weights:
+                for p in range(3):
+                    relay(w, p, 0).start()
                 take(w).wait()
                 put(w).start()
 
@@ -87,14 +109,18 @@
                 put(w).wait()
             for p in range(3):
                 copy(w, p, stage - 1).wait_recv()
-                copy(w, p, stage).start()
+                if stage < 3:
+                    copy(w, p, stage).start()
+                relay(w, p, stage).start()
 
         def last():
             for w in weights:
                 for p in range(3):
-                    copy(w, p, 3).wait_recv()
                     for stage in range(4):
-                        copy(w, p, stage).wait_send()
+                        relay(w, p, stage).wait_recv()
+                        relay(w, p, stage).wait_send()
+                        if stage < 3:
+                            copy(w, p, stage).wait_send()
 
         middle = [functools.partial(later, w, stage) for stage in (1, 2, 3) for w in weights]
         return [first, *middle, last]
@@ -103,6 +129,7 @@
 class Scatter:
     def __init__(self, *terms):
         n = self.n = len(terms)
+        terms, self.shifts = zip(*terms)
         self.inputs = terms
         shapes = [t.shape[4:] for t in terms]
         self.cols = [PARTS[s[1]] for s in shapes]
@@ -112,7 +139,10 @@
         self.scratch = []
         for s in shapes:
             self.scratch += [pltpu.VMEM((*(2,) * lead, *s), BF16) for lead in (3, 3, 2, 1, 0)]
-        self.scratch += [dma((n, 2)), dma((n, 2)), dma((n, 3, 3)), dma((n, 3, 3))]
+        self.scratch += [dma((n, 2)), dma((n, 3, 4)), dma((n, 3, 3)), dma((n, 3, 3))]
+
+    def order(self, w, p):
+        return ORDERS[(p + self.shifts[w]) % 3]
 
     def events(self, terms, sums, scratch):
         held = [scratch[5 * w : 5 * w + 5] for w in range(self.n)]
@@ -121,8 +151,13 @@
         cube = at[:3]
         items = [(w, p) for w in range(self.n) for p in range(3)]
 
-        def swap(w):
-            return remote(terms[w].at[BOTH, BOTH, BOTH, 1 - at[3]], held[w][1], core.at[w, 0], core.at[w, 1], 3)
+        def swap(w, p, near):
+            first = self.order(w, p)[0]
+            index = [BOTH, BOTH, BOTH]
+            index[first] = cube[first] if near else 1 - cube[first]
+            src = terms[w].at[(*index, 1 - at[3], slice(None), columns(w, p))]
+            dst = held[w][1].at[(*index, slice(None), columns(w, p))]
+            return remote(src, dst, core.at[w, p, 2 * near], core.at[w, p, 2 * near + 1], 3)
 
         def take(w):
             return pltpu.make_async_copy(terms[w].at[BOTH, BOTH, BOTH, at[3]], held[w][0], local.at[w, 0])
@@ -134,7 +169,7 @@
             return pl.ds(*self.cols[w][p])
 
         def copy(w, p, stage):
-            order = ORDERS[p]
+            order = self.order(w, p)
             index = list(cube)
             index[order[stage]] = 1 - cube[order[stage]]
             for a in order[stage + 1 :]:
@@ -144,7 +179,7 @@
             return remote(src, dst, send.at[w, p, stage], recv.at[w, p, stage], order[stage])
 
         def add(w, p, stage):
-            order = ORDERS[p]
+            order = self.order(w, p)
             free = order[stage + 1 :] if stage < 3 else ()
             chunk = 32 if self.rows[w] % 32 == 0 else 16
             for number in range(2 ** len(free)):
@@ -165,15 +200,19 @@
                 pl.loop(0, self.rows[w] // chunk)(some_rows)
 
         def first():
-            for w in range(self.n):
-                swap(w).start()
-                take(w).start()
+            for near in (0, 1):
+                for w in range(self.n):
+                    for p in range(3):
+                        swap(w, p, near).start()
+                    if not near:
+                        take(w).start()
 
         def leave(w, stage):
             if stage == 0:
                 take(w).wait()
-                swap(w).wait_recv()
             for p in range(3):
+                if stage < 2:
+                    swap(w, p, stage).wait_recv()
                 if stage > 0:
                     copy(w, p, stage - 1).wait_recv()
                 add(w, p, stage)
@@ -184,8 +223,9 @@
 
         def last():
             for w in range(self.n):
-                swap(w).wait_send()
                 for p in range(3):
+                    swap(w, p, 0).wait_send()
+                    swap(w, p, 1).wait_send()
                     for stage in range(3):
                         copy(w, p, stage).wait_send()
                 put(w).wait()
@@ -194,7 +234,7 @@
         return [first, *middle, last]
 
 
-def call(name, body, steps, inputs, in_specs, out_shapes, out_specs, flops=0, scratch=(), side=None, when=(), number=None):
+def call(name, body, steps, inputs, in_specs, out_shapes, out_specs, flops=0, scratch=(), aliases=None, side=None, when=(), number=None):
     n_in, n_out, n_scratch = len(inputs), len(out_shapes), len(scratch)
     s_in, s_out = (len(side.inputs), len(side.out_shapes)) if side else (0, 0)
 
@@ -235,6 +275,7 @@
         out_specs=[*out_specs, *[ANY] * s_out],
         out_shape=[*out_shapes, *(side.out_shapes if side else ())],
         scratch_shapes=[*scratch, *(side.scratch if side else ())],
+        input_output_aliases=aliases or {},
         compiler_params=pltpu.CompilerParams(**params),
         cost_estimate=pl.CostEstimate(flops=flops, bytes_accessed=0, transcendentals=0),
     )(*inputs, *(side.inputs if side else ()))
@@ -323,56 +364,65 @@
     return (d * u * (s + gs * (1 - s))).astype(BF16), (d * gs).astype(BF16), (gs * u).astype(BF16)
 
 
-def turn_body(a, dy, wg, wu, wd, hid, dgate, dup):
+def grads(r_at, r_dy, dgate, dup, hid, gd, gg, gu):
+    gg[...] = dot(r_at[...], dgate[...]).astype(BF16)
+    gu[...] = dot(r_at[...], dup[...]).astype(BF16)
+    gd[...] = dot(hid[...], r_dy[...], TN).astype(BF16)
+
+
+def turn_body(a, at, dy, wg, wu, wd, *refs):
+    dgate, dup, gd, gg, gu, hid = refs[-6:]
     for r in chunks(256):
         g, u = dot(a[r, :], wg[...]), dot(a[r, :], wu[...])
         d = dot(dy[r, :], wd[...], NT).astype(BF16).astype(F32)
         dgate[r, :], dup[r, :], hid[r, :] = gated_back(g, u, d)
-
-
-def turn(a, dy, wg, wu, wd, **side):
-    n = 256
+    grads(at, dy, dgate, dup, hid, gd, gg, gu)
+
+
+def turn(a, at, dy, wg, wu, wd, first, tiles, so_far=(), **side):
+    n = 256
+    columns = pl.BlockSpec((T, n), lambda i: (0, first + i))
+    rows = pl.BlockSpec((n, D), lambda i: (first + i, 0))
     return call(
-        "turn", turn_body, FF // n, [a, dy, wg, wu, wd],
-        [kept(T, D), kept(T, D), across(D, n), across(D, n), down(n, D)],
-        [shape(T, FF)] * 3, [across(T, n)] * 3, flops=3 * MM, **side,
-    )
-
-
-def hidden_back_body(dh, wd, gate, up, dgate, dup):
+        f"turn_{first}", turn_body, tiles, [a, at, dy, wg, wu, wd, *so_far],
+        [kept(T, D), kept(D, T), kept(T, D), across(D, n), across(D, n), rows, *[ANY] * len(so_far)],
+        [shape(T, FF), shape(T, FF), shape(FF, D), shape(D, tiles * n), shape(D, tiles * n)],
+        [columns, columns, rows, across(D, n), across(D, n)],
+        flops=6 * MM * tiles // 11, scratch=[pltpu.VMEM((T, n), BF16)],
+        aliases={6 + k: k for k in range(len(so_far))}, **side,
+    )
+
+
+def hidden_back_body(at, dh, wd, gate, up, *refs):
+    dgate, dup, gd, gg, gu, hid = refs[-6:]
     for r in chunks(256):
         d = dot(dh[r, :], wd[...], NT).astype(BF16).astype(F32)
-        dgate[r, :], dup[r, :], _ = gated_back(gate[r, :], up[r, :], d)
-
-
-def hidden_back(dh, wd, gate, up, **side):
-    n = 256
+        dgate[r, :], dup[r, :], hid[r, :] = gated_back(gate[r, :], up[r, :], d)
+    grads(at, dh, dgate, dup, hid, gd, gg, gu)
+
+
+def hidden_back(at, dh, wd, gate, up, first, tiles, so_far=(), **side):
+    n = 256
+    columns = pl.BlockSpec((T, n), lambda i: (0, first + i))
+    rows = pl.BlockSpec((n, D), lambda i: (first + i, 0))
     return call(
-        "hidden_back", hidden_back_body, FF // n, [dh, wd, gate, up],
-        [kept(T, D), down(n, D), across(T, n), across(T, n)], [shape(T, FF)] * 2, [across(T, n)] * 2, flops=MM, **side,
-    )
-
-
-def grad_down_body(hid, dy, out):
-    out[...] = dot(hid[...], dy[...], TN).astype(BF16)
-
-
-def grad_down(hid, dy, **side):
-    n = 256
-    return call("grad_down", grad_down_body, FF // n, [hid, dy], [across(T, n), kept(T, D)], [shape(FF, D)], [down(n, D)], flops=MM, **side)
-
-
-def grad_in_body(at, d, out):
-    out[...] = dot(at[...], d[...]).astype(BF16)
-
-
-def grad_in(at, d, **side):
-    n = 256
-    return call("grad_in", grad_in_body, FF // n, [at, d], [kept(D, T), across(T, n)], [shape(D, FF)], [across(D, n)], flops=MM, **side)
-
-
-def back_body(dg, du, wg, wu, h, dy, out):
-    da = (dot(dg[...], wg[...], NT) + dot(du[...], wu[...], NT)).astype(BF16).astype(F32)
+        f"hidden_back_{first}", hidden_back_body, tiles, [at, dh, wd, gate, up, *so_far],
+        [kept(D, T), kept(T, D), rows, columns, columns, *[ANY] * len(so_far)],
+        [shape(T, FF), shape(T, FF), shape(FF, D), shape(D, tiles * n), shape(D, tiles * n)],
+        [columns, columns, rows, across(D, n), across(D, n)],
+        flops=4 * MM * tiles // 11, scratch=[pltpu.VMEM((T, n), BF16)],
+        aliases={5 + k: k for k in range(len(so_far))}, **side,
+    )
+
+
+def back_body(dg, du, h, dy, *refs):
+    *weights, out = refs
+    half, start, da = len(weights) // 2, 0, 0
+    for wg, wu in zip(weights[:half], weights[half:]):
+        k = slice(start, start + wg.shape[1])
+        da += dot(dg[:, k], wg[...], NT) + dot(du[:, k], wu[...], NT)
+        start += wg.shape[1]
+    da = da.astype(BF16).astype(F32)
     wide = h[...].astype(F32)
     s = scale_of(wide)
     through = jnp.sum(da * wide, -1, keepdims=True)
@@ -381,9 +431,10 @@
 
 def back(dg, du, wg, wu, h, dy, **side):
     n = 256
+    weights = [*wg, *wu]
     return call(
-        "back", back_body, T // n, [dg, du, wg, wu, h, dy],
-        [down(n, FF), down(n, FF), kept(D, FF), kept(D, FF), down(n, D), down(n, D)],
+        "back", back_body, T // n, [dg, du, h, dy, *weights],
+        [down(n, FF), down(n, FF), down(n, D), down(n, D), *[kept(*w.shape) for w in weights]],
         [shape(T, D)], [down(n, D)], flops=2 * MM, **side,
     )
 
@@ -395,24 +446,45 @@
 def device_step(x, dy, w_gate, w_up, w_down):
     x, dy = x.reshape(T, D), dy.reshape(T, D)
 
-    a0, a0t, wg0, wu0, wd0 = norm(x, side=Gather(0, w_gate, w_up, w_down), when=(0, 2, 3, 4), number=1)
-    wg0, wu0, wd0 = wg0.reshape(D, FF), wu0.reshape(D, FF), wd0.reshape(FF, D)
-    gate0, up0, hid0, wg1, wu1 = gate_up(a0, wg0, wu0, side=Gather(1, w_gate, w_up), when=(0, 1, 2, 4, 6, 10), number=2)
-    h1, a1, a1t, wd1 = down_norm(hid0, wd0, x, side=Gather(1, w_down), when=(0, 2, 4), number=3)
-    wg1, wu1, wd1 = wg1.reshape(D, FF), wu1.reshape(D, FF), wd1.reshape(FF, D)
-
-    hid1, dgate1, dup1 = turn(a1, dy, wg1, wu1, wd1)
-    (gd1,) = grad_down(hid1, dy)
-    gg1, sd1 = grad_in(a1t, dgate1, side=Scatter(blocks_of(gd1)), when=(0, 4), number=4)
-    (gu1,) = grad_in(a1t, dup1)
-    dh1, sg1, su1 = back(dgate1, dup1, wg1, wu1, h1, dy, side=Scatter(blocks_of(gg1), blocks_of(gu1)), when=(0, 2, 3, 5, 7), number=5)
-
-    (gd0,) = grad_down(hid0, dh1)
-    dgate0, dup0, sd0 = hidden_back(dh1, wd0, gate0, up0, side=Scatter(blocks_of(gd0)), when=(0, 3, 6, 9), number=6)
-    (gg0,) = grad_in(a0t, dgate0)
-    gu0, sg0 = grad_in(a0t, dup0, side=Scatter(blocks_of(gg0)), when=(0, 4), number=7)
-    dx, su0 = back(dgate0, dup0, wg0, wu0, x, dh1, side=Scatter(blocks_of(gu0)), when=(0, 2, 5, 7), number=8)
-    return dx[None], jnp.stack([sg0, sg1]), jnp.stack([su0, su1]), jnp.stack([sd0, sd1])
+    first, rest = 1536, 1280
+    a0, a0t, wg0, wu0 = norm(x, side=Gather((w_gate, 0, 0, FF, 0), (w_up, 0, 0, FF, 1)), when=(0, 3, 5), number=1)
+    wg0, wu0 = wg0.reshape(D, FF), wu0.reshape(D, FF)
+    gate0, up0, hid0, wd0, wd1 = gate_up(
+        a0, wg0, wu0, side=Gather((w_down, 0, 0, D, 0), (w_down, 1, 0, D, 1)), when=(0, 2, 2, 4, 6, 10), number=2
+    )
+    wd0, wd1 = wd0.reshape(FF, D), wd1.reshape(FF, D)
+    h1, a1, a1t, wg1a, wu1a = down_norm(
+        hid0, wd0, x, side=Gather((w_gate, 1, 0, first, 0), (w_up, 1, 0, first, 1)), when=(0, 2, 2, 4, 5), number=3
+    )
+    wg1a, wu1a = wg1a.reshape(D, first), wu1a.reshape(D, first)
+
+    *so_far, gg1a, gu1a, wg1b, wu1b = turn(
+        a1, a1t, dy, wg1a, wu1a, wd1, 0, 6,
+        side=Gather((w_gate, 1, first, rest, 0), (w_up, 1, first, rest, 1)), when=(0, 1, 1, 2, 2, 4, 4, 5), number=4,
+    )
+    wg1b, wu1b = wg1b.reshape(D, rest), wu1b.reshape(D, rest)
+    dgate1, dup1, gd1, gg1b, gu1b, sg1a, su1a = turn(
+        a1, a1t, dy, wg1b, wu1b, wd1, 6, 5, so_far,
+        side=Scatter((blocks_of(gg1a), 0), (blocks_of(gu1a), 1)), when=(0, 1, 1, 3, 3, 4, 4), number=5,
+    )
+    dh1, sd1 = back(
+        dgate1, dup1, [wg1a, wg1b], [wu1a, wu1b], h1, dy, side=Scatter((blocks_of(gd1), 0)), when=(0, 1, 4, 6, 7), number=6
+    )
+    *so_far, gg0a, gu0a, sg1b, su1b = hidden_back(
+        a0t, dh1, wd0, gate0, up0, 0, 6,
+        side=Scatter((blocks_of(gg1b), 0), (blocks_of(gu1b), 1)), when=(0, 1, 1, 3, 3, 4, 4, 5, 5), number=7,
+    )
+    dgate0, dup0, gd0, gg0b, gu0b, sg0a, su0a = hidden_back(
+        a0t, dh1, wd0, gate0, up0, 6, 5, so_far,
+        side=Scatter((blocks_of(gg0a), 0), (blocks_of(gu0a), 1)), when=(0, 1, 1, 3, 3, 4, 4), number=8,
+    )
+    dx, sd0, sg0b, su0b = back(
+        dgate0, dup0, [wg0], [wu0], x, dh1,
+        side=Scatter((blocks_of(gd0), 0), (blocks_of(gg0b), 2), (blocks_of(gu0b), 2)), when=(0, 1, 2, 2, 5, 6, 7), number=9,
+    )
+    sg = jnp.stack([jnp.concatenate(pair, 1) for pair in ((sg0a, sg0b), (sg1a, sg1b))])
+    su = jnp.stack([jnp.concatenate(pair, 1) for pair in ((su0a, su0b), (su1a, su1b))])
+    return dx[None], sg, su, jnp.stack([sd0, sd1])
 
 
 def solution(mesh):

time: 497 us -> 409 us (0.82)
  Pallas kernels: 485 us -> 400 us
    pallas_call x13 -> x9, Pallas kernels: 485 us -> 400 us  [call(): pl.pallas_call(kernel, name=name, grid=(steps,), in_specs=[*in_specs, *[A...]
where the time goes in v3:
time: 409 us; the launch traced here: 408 us
  Pallas kernels  400 us (98%)
  other arithmetic  5.28 us (1%)
    pallas_call x9, Pallas kernels, call(): pl.pallas_call(kernel, name=name, grid=(steps,), in_specs=[*in_specs, *[A...  400 us

profile of v3, /device:TPU:0, one launch (start us, length us, event | category | flops | bytes accessed | tf_op | source)
XLA Modules:
  0.0 408.5 jit_solution(5003090709492006556)
XLA Ops:
  0.6 47.1 %norm.1 = (bf16[2048,1024]{1,0:T(8,128)(2,1)}, bf16[1024,2048]{1,0:T(8,128)(2,1)}, bf16[2,2,2,2,64,2816]{5,4,3,2,1,0:T(8,128)(2,1)}, bf16[2,2,2,2,64,2816]{5,4,3,2,1,0:T(8,128)(2,1)}) custom-call(bf16[2048,1024]{1,0:T(8,128)(2,1)} %bitcast.35, bf16[2,64,2816]{2,1,0:T(8,128)(2,1)} %refs_6_.1, bf16[2,64,2816]{2,1,0:T(8,128)(2,1)} %refs_7_.1), custom_call_target="tpu_custom_call" | custom-call | tf_op jit(solution)/shard_map/norm/pallas_call | solution.py:270
  47.7 50.6 %gate_up.1 = (f32[2048,2816]{1,0:T(8,128)}, f32[2048,2816]{1,0:T(8,128)}, bf16[2048,2816]{1,0:T(8,128)(2,1)}, bf16[2,2,2,2,176,1024]{5,4,3,2,1,0:T(8,128)(2,1)}, bf16[2,2,2,2,176,1024]{5,4,3,2,1,0:T(8,128)(2,1)}) custom-call(bf16[2048,1024]{1,0:T(8,128)(2,1)} %get-tuple-element.53.refs_0_, bf16[1024,2816]{1,0:T(8,128)(2,1)} %bitcast.43, ...), custom_call_target="tpu_custom_call" | custom-call | flops 23622320128 | tf_op jit(solution)/shard_map/gate_up/pallas_call | solution.py:270
  98.4 32.4 %down.1 = (bf16[2048,1024]{1,0:T(8,128)(2,1)}, bf16[2048,1024]{1,0:T(8,128)(2,1)}, bf16[1024,2048]{1,0:T(8,128)(2,1)}, bf16[2,2,2,2,64,1536]{5,4,3,2,1,0:T(8,128)(2,1)}, bf16[2,2,2,2,64,1536]{5,4,3,2,1,0:T(8,128)(2,1)}) custom-call(bf16[2048,2816]{1,0:T(8,128)(2,1)} %get-tuple-element.56.refs_0_, bf16[2816,1024]{1,0:T(8,128)(2,1)} %bitcast.31, ...), custom_call_target="tpu_custom_call" | custom-call | flops 11811160064 | tf_op jit(solution)/shard_map/down/pallas_call | solution.py:270
  130.8 51.0 %turn_0.1 = (bf16[2048,2816]{1,0:T(8,128)(2,1)}, bf16[2048,2816]{1,0:T(8,128)(2,1)}, bf16[2816,1024]{1,0:T(8,128)(2,1)}, bf16[1024,1536]{1,0:T(8,128)(2,1)}, bf1...) custom-call(bf16[2048,1024]{1,0:T(8,128)(2,1)} %get-tuple-element.58.refs, ...), custom_call_target="tpu_custom_call" | custom-call | flops 38654705664 | tf_op jit(solution)/shard_map/turn_0/pallas_call | solution.py:270
  181.8 46.0 %turn_6.1 = (bf16[2048,2816]{1,0:T(8,128)(2,1)}, bf16[2048,2816]{1,0:T(8,128)(2,1)}, bf16[2816,1024]{1,0:T(8,128)(2,1)}, bf16[1024,1280]{1,0:T(8,128)(2,1)}, bf1...) custom-call(bf16[2048,1024]{1,0:T(8,128)(2,1)} %get-tuple-element.58, ...), custom_call_target="tpu_custom_call", output_to_operand_aliasing={{0}: (6, {}), {1}: (7, {}), {2}: (8, {})} | custom-call | flops 32212254720 | tf_op jit(solution)/shard_map/turn_6/pallas_call | solution.py:270
  227.8 40.6 %back.2 = (bf16[2048,1024]{1,0:T(8,128)(2,1)}, bf16[176,1024]{1,0:T(8,128)(2,1)}) custom-call(bf16[2048,2816]{1,0:T(8,128)(2,1)} %get-tuple-element.70.refs_0_, bf16[2048,2816]{1,0:T(8,128)(2,1)} %get-tuple-element.71.refs_1_, bf16[2048,1024]{1,0:T(8,128)(2,1)} %get-tuple-element.72.refs_2_, bf16[2048,1024]{1,0:T(8,128)(2,1)} %bitcast.49, ...), custom_call_target="tpu_custom_call" | custom-call | flops 23622320128 | tf_op jit(solution)/shard_map/back/pallas_call | solution.py:270
  268.5 42.7 %hidden_back_0.1 = (bf16[2048,2816]{1,0:T(8,128)(2,1)}, bf16[2048,2816]{1,0:T(8,128)(2,1)}, bf16[2816,1024]{1,0:T(8,128)(2,1)}, bf16[1024,1536]{1,0:T(8,128)(2,1...) custom-call(bf16[1024,2048]{1,0:T(8,128)(2,1)} %get-tuple-element.52.refs_0_, ...), custom_call_target="tpu_custom_call" | custom-call | flops 25769803776 | tf_op jit(solution)/shard_map/hidden_back_0/pallas_call | solution.py:270
  311.2 39.3 %hidden_back_6.1 = (bf16[2048,2816]{1,0:T(8,128)(2,1)}, bf16[2048,2816]{1,0:T(8,128)(2,1)}, bf16[2816,1024]{1,0:T(8,128)(2,1)}, bf16[1024,1280]{1,0:T(8,128)(2,1...) custom-call(bf16[1024,2048]{1,0:T(8,128)(2,1)} %get-tuple-element.52, ...), custom_call_target="tpu_custom_call", output_to_operand_aliasing={{0}: (5, {}), {1}: (6, {}), {2}: (7, {})} | custom-call | flops 21474836480 | tf_op jit(solution)/shard_map/hidden_back_6/pallas_call | solution.py:270
  350.5 0.0 copy-start.5
  350.5 0.0 copy-start.6
  350.5 0.0 copy-start.3
  350.5 0.0 copy-start.4
  350.5 0.0 copy-start.7
  350.5 50.6 %back.3 = (bf16[2048,1024]{1,0:T(8,128)(2,1)}, bf16[176,1024]{1,0:T(8,128)(2,1)}, bf16[64,1280]{1,0:T(8,128)(2,1)}, bf16[64,1280]{1,0:T(8,128)(2,1)}) custom-call(bf16[2048,2816]{1,0:T(8,128)(2,1)} %get-tuple-element.84.refs_0_, bf16[2048,2816]{1,0:T(8,128)(2,1)} %get-tuple-element.85.refs_1_, bf16[2048,1024]{1,0:T(8,128)(2,1)} %bitcast.37, ...), custom_call_target="tpu_custom_call" | custom-call | flops 23622320128 | tf_op jit(solution)/shard_map/back/pallas_call | solution.py:270
  401.1 0.0 copy-start.1
  401.1 0.0 copy-start.2
  401.1 0.0 copy-start
  401.1 0.0 copy-done.5
  401.1 0.0 copy-done.6
  401.1 1.2 maximum_bitcast_fusion
  402.3 0.0 copy-done.3
  402.4 0.0 copy-done.4
  402.4 0.0 copy-done.7
  402.4 1.3 maximum_bitcast_fusion.1
  403.7 0.9 pad_maximum_fusion
  404.6 0.9 pad_maximum_fusion.1
  405.5 0.0 copy-done.1
  405.5 0.0 copy-done.2
  405.5 0.9 pad_maximum_fusion.2
  406.5 0.0 copy-done
  406.5 2.0 copy.22
Async XLA Ops:
  350.5 50.7 %copy-start.5 = (bf16[64,1536]{1,0:T(8,128)(2,1)S(1)}, bf16[64,1536]{1,0:T(8,128)(2,1)}, u32[]{:S(2)}) copy-start(bf16[64,1536]{1,0:T(8,128)(2,1)} %get-tuple-element.90) | copy-start | bytes 589828
  350.5 50.7 %copy-start.6 = (bf16[64,1536]{1,0:T(8,128)(2,1)S(1)}, bf16[64,1536]{1,0:T(8,128)(2,1)}, u32[]{:S(2)}) copy-start(bf16[64,1536]{1,0:T(8,128)(2,1)} %get-tuple-element.94) | copy-start | bytes 589828
  350.5 51.9 %copy-start.3 = (bf16[64,1536]{1,0:T(8,128)(2,1)S(1)}, bf16[64,1536]{1,0:T(8,128)(2,1)}, u32[]{:S(2)}) copy-start(bf16[64,1536]{1,0:T(8,128)(2,1)} %get-tuple-element.92) | copy-start | bytes 589828
  350.5 51.9 %copy-start.4 = (bf16[64,1536]{1,0:T(8,128)(2,1)S(1)}, bf16[64,1536]{1,0:T(8,128)(2,1)}, u32[]{:S(2)}) copy-start(bf16[64,1536]{1,0:T(8,128)(2,1)} %get-tuple-element.96) | copy-start | bytes 589828
  350.5 51.9 %copy-start.7 = (bf16[64,1280]{1,0:T(8,128)(2,1)S(1)}, bf16[64,1280]{1,0:T(8,128)(2,1)}, u32[]{:S(2)}) copy-start(bf16[64,1280]{1,0:T(8,128)(2,1)} %get-tuple-element.93) | copy-start | bytes 491524
  401.1 4.4 %copy-start.1 = (bf16[176,1024]{1,0:T(8,128)(2,1)S(1)}, bf16[176,1024]{1,0:T(8,128)(2,1)}, u32[]{:S(2)}) copy-start(bf16[176,1024]{1,0:T(8,128)(2,1)} %get-tuple-element.99) | copy-start | bytes 1081348
  401.1 4.4 %copy-start.2 = (bf16[176,1024]{1,0:T(8,128)(2,1)S(1)}, bf16[176,1024]{1,0:T(8,128)(2,1)}, u32[]{:S(2)}) copy-start(bf16[176,1024]{1,0:T(8,128)(2,1)} %get-tuple-element.98) | copy-start | bytes 1081348
  401.1 5.3 %copy-start = (bf16[2048,1024]{1,0:T(8,128)(2,1)S(1)}, bf16[2048,1024]{1,0:T(8,128)(2,1)}, u32[]{:S(2)}) copy-start(bf16[2048,1024]{1,0:T(8,128)(2,1)} %get-tuple-element.89) | copy-start | bytes 12582916

commit v4 on v3

--- a/solution.py
+++ b/solution.py
@@ -50,6 +50,9 @@
 
 
 class Gather:
+    aliases = {}
+
+
     def __init__(self, *weights):
         n = self.n = len(weights)
         self.inputs, self.layers, self.starts, sizes, self.shifts = zip(*weights)
@@ -129,12 +132,14 @@
 class Scatter:
     def __init__(self, *terms):
         n = self.n = len(terms)
-        terms, self.shifts = zip(*terms)
-        self.inputs = terms
+        terms, self.shifts, results, self.layers, self.starts = zip(*terms)
+        so_far = [w for w in range(n) if not isinstance(results[w], jax.ShapeDtypeStruct)]
+        self.inputs = [*terms, *[results[w] for w in so_far]]
+        self.aliases = {n + k: w for k, w in enumerate(so_far)}
         shapes = [t.shape[4:] for t in terms]
         self.cols = [PARTS[s[1]] for s in shapes]
         self.rows = [s[0] for s in shapes]
-        self.out_shapes = [jax.ShapeDtypeStruct(s, BF16) for s in shapes]
+        self.out_shapes = [jax.ShapeDtypeStruct(r.shape, BF16) for r in results]
         dma = pltpu.SemaphoreType.DMA
         self.scratch = []
         for s in shapes:
@@ -163,7 +168,9 @@
             return pltpu.make_async_copy(terms[w].at[BOTH, BOTH, BOTH, at[3]], held[w][0], local.at[w, 0])
 
         def put(w):
-            return pltpu.make_async_copy(held[w][0].at[tuple(cube)], sums[w], local.at[w, 1])
+            mine = held[w][0].at[tuple(cube)]
+            where = (self.layers[w], slice(None), pl.ds(self.starts[w], mine.shape[1]))
+            return pltpu.make_async_copy(mine, sums[w].at[where], local.at[w, 1])
 
         def columns(w, p):
             return pl.ds(*self.cols[w][p])
@@ -181,23 +188,28 @@
         def add(w, p, stage):
             order = self.order(w, p)
             free = order[stage + 1 :] if stage < 3 else ()
-            chunk = 32 if self.rows[w] % 32 == 0 else 16
+            indices = []
             for number in range(2 ** len(free)):
                 index = list(cube)
                 if stage < 3:
                     index[order[stage]] = 1 - cube[order[stage]]
                 for k, a in enumerate(free):
                     index[a] = (number >> k) & 1
-
-                def some_rows(i, index=index):
-                    where = (pl.ds(pl.multiple_of(i * chunk, chunk), chunk), columns(w, p))
+                indices.append(index)
+
+            def some_rows(i):
+                where = (pl.ds(pl.multiple_of(i * 16, 16), 16), columns(w, p))
+                totals = []
+                for index in indices:
                     total = held[w][0][(*index, *where)].astype(F32) + held[w][1][(*index, *where)].astype(F32)
                     for j in range(stage):
                         rest = [index[a] for a in range(3) if a not in order[: j + 1]]
                         total += held[w][2 + j][(*rest, *where)].astype(F32)
-                    held[w][0][(*index, *where)] = total.astype(BF16)
-
-                pl.loop(0, self.rows[w] // chunk)(some_rows)
+                    totals.append(total.astype(BF16))
+                for index, total in zip(indices, totals):
+                    held[w][0][(*index, *where)] = total
+
+            pl.loop(0, self.rows[w] // 16)(some_rows)
 
         def first():
             for near in (0, 1):
@@ -234,17 +246,35 @@
         return [first, *middle, last]
 
 
-def call(name, body, steps, inputs, in_specs, out_shapes, out_specs, flops=0, scratch=(), aliases=None, side=None, when=(), number=None):
+def call(name, body, steps, inputs, in_specs, out_shapes, out_specs, flops=0, late=(), scratch=(), aliases=None, side=None, when=(), number=None):
     n_in, n_out, n_scratch = len(inputs), len(out_shapes), len(scratch)
     s_in, s_out = (len(side.inputs), len(side.out_shapes)) if side else (0, 0)
+    n_late = len(late)
 
     def kernel(*refs):
         ins, refs = refs[:n_in], refs[n_in:]
         side_ins, refs = refs[:s_in], refs[s_in:]
+        late_ins, refs = refs[:n_late], refs[n_late:]
         outs, refs = refs[:n_out], refs[n_out:]
         side_outs, refs = refs[:s_out], refs[s_out:]
-        own, side_scratch = refs[:n_scratch], refs[n_scratch:]
+        own, refs = refs[:n_scratch], refs[n_scratch:]
+        held, refs = refs[:n_late], refs[n_late:]
+        (late_sem, side_scratch) = (refs[0], refs[1:]) if late else (None, refs)
         step = pl.program_id(0)
+
+        def fetch(k):
+            return pltpu.make_async_copy(late_ins[k], held[k], late_sem.at[k])
+
+        def ready(k):
+            pl.when(step == 0)(lambda: fetch(k).wait())
+
+        if late:
+
+            def fetch_all():
+                for k in range(n_late):
+                    fetch(k).start()
+
+            pl.when(step == 0)(fetch_all)
         events = side.events(side_ins, side_outs, side_scratch) if side else []
         for k, event in enumerate(events):
             if k < len(when):
@@ -255,7 +285,7 @@
                     event()
 
                 pl.when(step == when[k])(now)
-        body(*ins, *outs, *own)
+        body(*ins, *outs, *own, *((held, ready) if late else ()))
         if len(events) > len(when):
 
             def end():
@@ -271,14 +301,19 @@
         kernel,
         name=name,
         grid=(steps,),
-        in_specs=[*in_specs, *[ANY] * s_in],
+        in_specs=[*in_specs, *[ANY] * (s_in + n_late)],
         out_specs=[*out_specs, *[ANY] * s_out],
         out_shape=[*out_shapes, *(side.out_shapes if side else ())],
-        scratch_shapes=[*scratch, *(side.scratch if side else ())],
-        input_output_aliases=aliases or {},
+        scratch_shapes=[
+            *scratch,
+            *[pltpu.VMEM(a.shape, a.dtype) for a in late],
+            *([pltpu.SemaphoreType.DMA((n_late,))] if late else []),
+            *(side.scratch if side else ()),
+        ],
+        input_output_aliases={**(aliases or {}), **({n_in + i: n_out + o for i, o in side.aliases.items()} if side else {})},
         compiler_params=pltpu.CompilerParams(**params),
         cost_estimate=pl.CostEstimate(flops=flops, bytes_accessed=0, transcendentals=0),
-    )(*inputs, *(side.inputs if side else ()))
+    )(*inputs, *(side.inputs if side else ()), *late)
 
 
 def shape(*dims, dtype=BF16):
@@ -370,12 +405,14 @@
     gd[...] = dot(hid[...], r_dy[...], TN).astype(BF16)
 
 
-def turn_body(a, at, dy, wg, wu, wd, *refs):
-    dgate, dup, gd, gg, gu, hid = refs[-6:]
+def turn_body(a, wg, wu, wd, *refs):
+    *_, dgate, dup, gd, gg, gu, hid, (dy, at), ready = refs
+    ready(0)
     for r in chunks(256):
         g, u = dot(a[r, :], wg[...]), dot(a[r, :], wu[...])
         d = dot(dy[r, :], wd[...], NT).astype(BF16).astype(F32)
         dgate[r, :], dup[r, :], hid[r, :] = gated_back(g, u, d)
+    ready(1)
     grads(at, dy, dgate, dup, hid, gd, gg, gu)
 
 
@@ -384,20 +421,25 @@
     columns = pl.BlockSpec((T, n), lambda i: (0, first + i))
     rows = pl.BlockSpec((n, D), lambda i: (first + i, 0))
     return call(
-        f"turn_{first}", turn_body, tiles, [a, at, dy, wg, wu, wd, *so_far],
-        [kept(T, D), kept(D, T), kept(T, D), across(D, n), across(D, n), rows, *[ANY] * len(so_far)],
+        f"turn_{first}", turn_body, tiles, [a, wg, wu, wd, *so_far],
+        [kept(T, D), across(D, n), across(D, n), rows, *[ANY] * len(so_far)],
         [shape(T, FF), shape(T, FF), shape(FF, D), shape(D, tiles * n), shape(D, tiles * n)],
         [columns, columns, rows, across(D, n), across(D, n)],
-        flops=6 * MM * tiles // 11, scratch=[pltpu.VMEM((T, n), BF16)],
-        aliases={6 + k: k for k in range(len(so_far))}, **side,
-    )
-
-
-def hidden_back_body(at, dh, wd, gate, up, *refs):
-    dgate, dup, gd, gg, gu, hid = refs[-6:]
-    for r in chunks(256):
+        flops=6 * MM * tiles // 11, scratch=[pltpu.VMEM((T, n), BF16)], late=[dy, at],
+        aliases={4 + k: k for k in range(len(so_far))}, **side,
+    )
+
+
+def hidden_back_body(dh, wd, gate, up, *refs):
+    *_, dgate, dup, gd, gg, gu, hid, (at,), ready = refs
+
+    @pl.loop(0, 2)
+    def half(i):
+        r = pl.ds(pl.multiple_of(i * (T // 2), T // 2), T // 2)
         d = dot(dh[r, :], wd[...], NT).astype(BF16).astype(F32)
         dgate[r, :], dup[r, :], hid[r, :] = gated_back(gate[r, :], up[r, :], d)
+
+    ready(0)
     grads(at, dh, dgate, dup, hid, gd, gg, gu)
 
 
@@ -406,22 +448,24 @@
     columns = pl.BlockSpec((T, n), lambda i: (0, first + i))
     rows = pl.BlockSpec((n, D), lambda i: (first + i, 0))
     return call(
-        f"hidden_back_{first}", hidden_back_body, tiles, [at, dh, wd, gate, up, *so_far],
-        [kept(D, T), kept(T, D), rows, columns, columns, *[ANY] * len(so_far)],
+        f"hidden_back_{first}", hidden_back_body, tiles, [dh, wd, gate, up, *so_far],
+        [kept(T, D), rows, columns, columns, *[ANY] * len(so_far)],
         [shape(T, FF), shape(T, FF), shape(FF, D), shape(D, tiles * n), shape(D, tiles * n)],
         [columns, columns, rows, across(D, n), across(D, n)],
-        flops=4 * MM * tiles // 11, scratch=[pltpu.VMEM((T, n), BF16)],
-        aliases={5 + k: k for k in range(len(so_far))}, **side,
-    )
-
-
-def back_body(dg, du, h, dy, *refs):
-    *weights, out = refs
-    half, start, da = len(weights) // 2, 0, 0
-    for wg, wu in zip(weights[:half], weights[half:]):
-        k = slice(start, start + wg.shape[1])
-        da += dot(dg[:, k], wg[...], NT) + dot(du[:, k], wu[...], NT)
-        start += wg.shape[1]
+        flops=4 * MM * tiles // 11, scratch=[pltpu.VMEM((T, n), BF16)], late=[at],
+        aliases={4 + k: k for k in range(len(so_far))}, **side,
+    )
+
+
+def back_body(dg, du, h, dy, out, weights, ready):
+    pieces = len(weights) // 2
+    for k, w in enumerate(weights):
+        if k % pieces == 0:
+            start = 0
+        d = (dg, du)[k // pieces][:, start : start + w.shape[1]]
+        start += w.shape[1]
+        ready(k)
+        da = dot(d, w[...], NT) + (da if k else 0)
     da = da.astype(BF16).astype(F32)
     wide = h[...].astype(F32)
     s = scale_of(wide)
@@ -431,11 +475,9 @@
 
 def back(dg, du, wg, wu, h, dy, **side):
     n = 256
-    weights = [*wg, *wu]
     return call(
-        "back", back_body, T // n, [dg, du, h, dy, *weights],
-        [down(n, FF), down(n, FF), down(n, D), down(n, D), *[kept(*w.shape) for w in weights]],
-        [shape(T, D)], [down(n, D)], flops=2 * MM, **side,
+        "back", back_body, T // n, [dg, du, h, dy], [down(n, FF), down(n, FF), down(n, D), down(n, D)],
+        [shape(T, D)], [down(n, D)], late=[*wg, *wu], flops=2 * MM, **side,
     )
 
 
@@ -446,45 +488,48 @@
 def device_step(x, dy, w_gate, w_up, w_down):
     x, dy = x.reshape(T, D), dy.reshape(T, D)
 
-    first, rest = 1536, 1280
     a0, a0t, wg0, wu0 = norm(x, side=Gather((w_gate, 0, 0, FF, 0), (w_up, 0, 0, FF, 1)), when=(0, 3, 5), number=1)
     wg0, wu0 = wg0.reshape(D, FF), wu0.reshape(D, FF)
-    gate0, up0, hid0, wd0, wd1 = gate_up(
-        a0, wg0, wu0, side=Gather((w_down, 0, 0, D, 0), (w_down, 1, 0, D, 1)), when=(0, 2, 2, 4, 6, 10), number=2
-    )
-    wd0, wd1 = wd0.reshape(FF, D), wd1.reshape(FF, D)
-    h1, a1, a1t, wg1a, wu1a = down_norm(
-        hid0, wd0, x, side=Gather((w_gate, 1, 0, first, 0), (w_up, 1, 0, first, 1)), when=(0, 2, 2, 4, 5), number=3
-    )
-    wg1a, wu1a = wg1a.reshape(D, first), wu1a.reshape(D, first)
+    grad = shape(2, D // 16, FF)
+    first, rest = 1280, 1536
+    gate0, up0, hid0, wd0, wg1a = gate_up(
+        a0, wg0, wu0, side=Gather((w_down, 0, 0, D, 0), (w_gate, 1, 0, first, 2)), when=(0, 1, 2, 4, 5, 9), number=2
+    )
+    wd0, wg1a = wd0.reshape(FF, D), wg1a.reshape(D, first)
+    h1, a1, a1t, wd1, wu1a = down_norm(
+        hid0, wd0, x, side=Gather((w_down, 1, 0, D, 0), (w_up, 1, 0, first, 2)), when=(0, 2, 2, 4, 6), number=3
+    )
+    wd1, wu1a = wd1.reshape(FF, D), wu1a.reshape(D, first)
 
     *so_far, gg1a, gu1a, wg1b, wu1b = turn(
-        a1, a1t, dy, wg1a, wu1a, wd1, 0, 6,
-        side=Gather((w_gate, 1, first, rest, 0), (w_up, 1, first, rest, 1)), when=(0, 1, 1, 2, 2, 4, 4, 5), number=4,
+        a1, a1t, dy, wg1a, wu1a, wd1, 0, 5,
+        side=Gather((w_gate, 1, first, rest, 0), (w_up, 1, first, rest, 1)), when=(0, 1, 1, 2, 2, 4, 4), number=4,
     )
     wg1b, wu1b = wg1b.reshape(D, rest), wu1b.reshape(D, rest)
-    dgate1, dup1, gd1, gg1b, gu1b, sg1a, su1a = turn(
-        a1, a1t, dy, wg1b, wu1b, wd1, 6, 5, so_far,
-        side=Scatter((blocks_of(gg1a), 0), (blocks_of(gu1a), 1)), when=(0, 1, 1, 3, 3, 4, 4), number=5,
-    )
-    dh1, sd1 = back(
-        dgate1, dup1, [wg1a, wg1b], [wu1a, wu1b], h1, dy, side=Scatter((blocks_of(gd1), 0)), when=(0, 1, 4, 6, 7), number=6
-    )
-    *so_far, gg0a, gu0a, sg1b, su1b = hidden_back(
+    dgate1, dup1, gd1, gg1b, gu1b, sg, su = turn(
+        a1, a1t, dy, wg1b, wu1b, wd1, 5, 6, so_far,
+        side=Scatter((blocks_of(gg1a), 0, grad, 1, 0), (blocks_of(gu1a), 1, grad, 1, 0)), when=(0, 1, 1, 3, 3, 4, 4, 5, 5), number=5,
+    )
+    dh1, sd = back(
+        dgate1, dup1, [wg1a, wg1b], [wu1a, wu1b], h1, dy,
+        side=Scatter((blocks_of(gd1), 0, shape(2, FF // 16, D), 1, 0)), when=(0, 1, 4, 6, 7), number=6,
+    )
+    *so_far, gg0a, gu0a, sg, su = hidden_back(
         a0t, dh1, wd0, gate0, up0, 0, 6,
-        side=Scatter((blocks_of(gg1b), 0), (blocks_of(gu1b), 1)), when=(0, 1, 1, 3, 3, 4, 4, 5, 5), number=7,
-    )
-    dgate0, dup0, gd0, gg0b, gu0b, sg0a, su0a = hidden_back(
+        side=Scatter((blocks_of(gg1b), 0, sg, 1, first), (blocks_of(gu1b), 1, su, 1, first)),
+        when=(0, 1, 1, 3, 3, 4, 4, 5, 5), number=7,
+    )
+    dgate0, dup0, gd0, gg0b, gu0b, sg, su = hidden_back(
         a0t, dh1, wd0, gate0, up0, 6, 5, so_far,
-        side=Scatter((blocks_of(gg0a), 0), (blocks_of(gu0a), 1)), when=(0, 1, 1, 3, 3, 4, 4), number=8,
-    )
-    dx, sd0, sg0b, su0b = back(
+        side=Scatter((blocks_of(gg0a), 0, sg, 0, 0), (blocks_of(gu0a), 1, su, 0, 0)), when=(0, 1, 1, 3, 3, 4, 4), number=8,
+    )
+    half = 6 * 256
+    dx, sd, sg, su = back(
         dgate0, dup0, [wg0], [wu0], x, dh1,
-        side=Scatter((blocks_of(gd0), 0), (blocks_of(gg0b), 2), (blocks_of(gu0b), 2)), when=(0, 1, 2, 2, 5, 6, 7), number=9,
-    )
-    sg = jnp.stack([jnp.concatenate(pair, 1) for pair in ((sg0a, sg0b), (sg1a, sg1b))])
-    su = jnp.stack([jnp.concatenate(pair, 1) for pair in ((su0a, su0b), (su1a, su1b))])
-    return dx[None], sg, su, jnp.stack([sd0, sd1])
+        side=Scatter((blocks_of(gd0), 0, sd, 0, 0), (blocks_of(gg0b), 2, sg, 0, half), (blocks_of(gu0b), 2, su, 0, half)),
+        when=(0, 1, 1, 2, 4, 5, 6), number=9,
+    )
+    return dx[None], sg, su, sd
 
 
 def solution(mesh):

time: 409 us -> 406 us (level)
  local copies, waits for them, and re-layouts: 2.05 us -> 7.38 us
  other arithmetic: 5.28 us -> 0 us
    unnamed x17 -> x10, local copies, waits for them, and re-layouts: 2.05 us -> 7.38 us
    another operation x5 -> x0, other arithmetic: 5.28 us -> none  [the longest x3 3.43 us: device_step(): jnp.stack([jnp.concatenate(pair, 1) for pair in ((sg0a, sg0b), (sg1a, sg1...]
where the time goes in v4:
time: 406 us; the launch traced here: 405 us
  Pallas kernels  397 us (98%)
  local copies, waits for them, and re-layouts  7.38 us (2%)
    pallas_call x9, Pallas kernels, call(): pl.pallas_call(kernel, name=name, grid=(steps,), in_specs=[*in_specs, *[A...  397 us

profile of v4, /device:TPU:0, one launch (start us, length us, event | category | flops | bytes accessed | tf_op | source)
XLA Modules:
  0.0 405.1 jit_solution(6089778802458061022)
XLA Ops:
  0.6 47.1 %norm.1 = (bf16[2048,1024]{1,0:T(8,128)(2,1)}, bf16[1024,2048]{1,0:T(8,128)(2,1)}, bf16[2,2,2,2,64,2816]{5,4,3,2,1,0:T(8,128)(2,1)}, bf16[2,2,2,2,64,2816]{5,4,3,2,1,0:T(8,128)(2,1)}) custom-call(bf16[2048,1024]{1,0:T(8,128)(2,1)} %bitcast.25, bf16[2,64,2816]{2,1,0:T(8,128)(2,1)} %refs_4_.5, bf16[2,64,2816]{2,1,0:T(8,128)(2,1)} %refs_5_.1), custom_call_target="tpu_custom_call" | custom-call | tf_op jit(solution)/shard_map/norm/pallas_call | solution.py:300
  47.8 41.1 %gate_up.1 = (f32[2048,2816]{1,0:T(8,128)}, f32[2048,2816]{1,0:T(8,128)}, bf16[2048,2816]{1,0:T(8,128)(2,1)}, bf16[2,2,2,2,176,1024]{5,4,3,2,1,0:T(8,128)(2,1)}, bf16[2,2,2,2,64,1280]{5,4,3,2,1,0:T(8,128)(2,1)}) custom-call(bf16[2048,1024]{1,0:T(8,128)(2,1)} %get-tuple-element.52.refs_0_, bf16[1024,2816]{1,0:T(8,128)(2,1)} %bitcast.31, ...), custom_call_target="tpu_custom_call" | custom-call | flops 23622320128 | tf_op jit(solution)/shard_map/gate_up/pallas_call | solution.py:300
  88.9 38.3 %down.1 = (bf16[2048,1024]{1,0:T(8,128)(2,1)}, bf16[2048,1024]{1,0:T(8,128)(2,1)}, bf16[1024,2048]{1,0:T(8,128)(2,1)}, bf16[2,2,2,2,176,1024]{5,4,3,2,1,0:T(8,128)(2,1)}, bf16[2,2,2,2,64,1280]{5,4,3,2,1,0:T(8,128)(2,1)}) custom-call(bf16[2048,2816]{1,0:T(8,128)(2,1)} %get-tuple-element.55.refs_0_, bf16[2816,1024]{1,0:T(8,128)(2,1)} %bitcast.21, ...), custom_call_target="tpu_custom_call" | custom-call | flops 11811160064 | tf_op jit(solution)/shard_map/down/pallas_call | solution.py:300
  127.2 46.2 %turn_0.1 = (bf16[2048,2816]{1,0:T(8,128)(2,1)}, bf16[2048,2816]{1,0:T(8,128)(2,1)}, bf16[2816,1024]{1,0:T(8,128)(2,1)}, bf16[1024,1280]{1,0:T(8,128)(2,1)}, bf1...) custom-call(bf16[2048,1024]{1,0:T(8,128)(2,1)} %get-tuple-element.57.refs, ...), custom_call_target="tpu_custom_call" | custom-call | flops 32212254720 | tf_op jit(solution)/shard_map/turn_0/pallas_call | solution.py:300
  173.4 52.7 %turn_5.1 = (bf16[2048,2816]{1,0:T(8,128)(2,1)}, bf16[2048,2816]{1,0:T(8,128)(2,1)}, bf16[2816,1024]{1,0:T(8,128)(2,1)}, bf16[1024,1536]{1,0:T(8,128)(2,1)}, bf1...) custom-call(bf16[2048,1024]{1,0:T(8,128)(2,1)} %get-tuple-element.57, ...), custom_call_target="tpu_custom_call", output_to_operand_aliasing={{0}: (4, {}), {1}: (5, {}), {2}: (6, {})} | custom-call | flops 38654705664 | tf_op jit(solution)/shard_map/turn_5/pallas_call | solution.py:300
  226.1 40.0 %back.2 = (bf16[2048,1024]{1,0:T(8,128)(2,1)}, bf16[2,176,1024]{2,1,0:T(8,128)(2,1)}) custom-call(bf16[2048,2816]{1,0:T(8,128)(2,1)} %get-tuple-element.69.refs_0_, bf16[2048,2816]{1,0:T(8,128)(2,1)} %get-tuple-element.70.refs_1_, bf16[2048,1024]{1,0:T(8,128)(2,1)} %get-tuple-element.71.refs_2_, bf16[2048,1024]{1,0:T(8,128)(2,1)} %bitcast.37, ...), custom_call_target="tpu_custom_call" | custom-call | flops 23622320128 | tf_op jit(solution)/shard_map/back/pallas_call | solution.py:300
  266.1 44.6 %hidden_back_0.1 = (bf16[2048,2816]{1,0:T(8,128)(2,1)}, bf16[2048,2816]{1,0:T(8,128)(2,1)}, bf16[2816,1024]{1,0:T(8,128)(2,1)}, bf16[1024,1536]{1,0:T(8,128)(2,1...) custom-call(bf16[2048,1024]{1,0:T(8,128)(2,1)} %get-tuple-element.73, ...), custom_call_target="tpu_custom_call", output_to_operand_aliasing={{5}: (6, {}), {6}: (7, {})} | custom-call | flops 25769803776 | tf_op jit(solution)/shard_map/hidden_back_0/pallas_call | solution.py:300
  310.7 39.3 %hidden_back_6.1 = (bf16[2048,2816]{1,0:T(8,128)(2,1)}, bf16[2048,2816]{1,0:T(8,128)(2,1)}, bf16[2816,1024]{1,0:T(8,128)(2,1)}, bf16[1024,1280]{1,0:T(8,128)(2,1...) custom-call(bf16[2048,1024]{1,0:T(8,128)(2,1)} %get-tuple-element.73, ...), custom_call_target="tpu_custom_call", output_to_operand_aliasing={{0}: (4, {}), {1}: (5, {}), {2}: (6, {}), {5}: (9, {}), {6}... | custom-call | flops 21474836480 | tf_op jit(solution)/shard_map/hidden_back_6/pallas_call | solution.py:300
  350.0 47.7 %back.3 = (bf16[2048,1024]{1,0:T(8,128)(2,1)}, bf16[2,176,1024]{2,1,0:T(8,128)(2,1)}, bf16[2,64,2816]{2,1,0:T(8,128)(2,1)}, bf16[2,64,2816]{2,1,0:T(8,128)(2,1)}) custom-call(bf16[2048,2816]{1,0:T(8,128)(2,1)} %get-tuple-element.88.refs_0_, bf16[2048,2816]{1,0:T(8,128)(2,1)} %get-tuple-element.89.refs_1_, ...), custom_call_target="tpu_custom_call", output_to_operand_aliasing={{1}: (7, {}), {2}: (8, {}), {3}: (9, {})} | custom-call | flops 23622320128 | tf_op jit(solution)/shard_map/back/pallas_call | solution.py:300
  397.7 0.0 copy-start
  397.7 0.0 copy-start.1
  397.7 0.0 copy-start.2
  397.7 4.8 %copy.39 = bf16[1,2048,1024]{2,1,0:T(8,128)(2,1)} copy(bf16[1,2048,1024]{2,1,0:T(8,128)(2,1)} %bitcast.28) | data formatting | bytes 8388608
  402.5 0.0 copy-done
  402.5 0.9 copy.40
  403.4 0.0 copy-done.1
  403.4 0.9 copy.41
  404.3 0.0 copy-done.2
  404.3 0.9 copy.42
Async XLA Ops:
  397.7 4.8 %copy-start = (bf16[2,64,2816]{2,1,0:T(8,128)(2,1)S(1)}, bf16[2,64,2816]{2,1,0:T(8,128)(2,1)}, u32[]{:S(2)}) copy-start(bf16[2,64,2816]{2,1,0:T(8,128)(2,1)} %get-tuple-element.105) | copy-start | bytes 2162692
  397.7 5.7 %copy-start.1 = (bf16[2,64,2816]{2,1,0:T(8,128)(2,1)S(1)}, bf16[2,64,2816]{2,1,0:T(8,128)(2,1)}, u32[]{:S(2)}) copy-start(bf16[2,64,2816]{2,1,0:T(8,128)(2,1)} %get-tuple-element.106) | copy-start | bytes 2162692
  397.7 6.5 %copy-start.2 = (bf16[2,176,1024]{2,1,0:T(8,128)(2,1)S(1)}, bf16[2,176,1024]{2,1,0:T(8,128)(2,1)}, u32[]{:S(2)}) copy-start(bf16[2,176,1024]{2,1,0:T(8,128)(2,1)} %get-tuple-element.107) | copy-start | bytes 2162692
